TPU v7x, 128 devices: a whole 4x4x4 slice. The times are simulated.
128 devices in a mesh: gx: 16 (over x, y), gy: 4 (over z_hi, core), gz: 2 (over z_lo).
Axes of the slice: x: 4, y: 4, z: 4 (z_hi: 2, z_lo: 2; z = z_hi * 2 + z_lo), core: 2. Of those that a mesh axis runs over, the one named last changes fastest.
Arguments:
- right_side: float32 [256, 256, 1024], P('gx', 'gy', 'gz'), may hold values from -24 to 24
- reaction: float32 [256, 256, 1024], P('gx', 'gy', 'gz'), may hold values from 0.5 to 2
- velocity: float32 [3, 256, 256, 1024], P(None, 'gx', 'gy', 'gz'), may hold values from -0.5 to 0.5
Outputs:
- solution: float32 [256, 256, 1024], P('gx', 'gy', 'gz')
- residual: float32 [256, 256, 1024], P('gx', 'gy', 'gz')
- residual_norm: float32 [], replicated
All inputs are finite; a program needn't handle non-finite values.
Results may differ from a plain program's by a relative error of at most 0.00002.
Values sent between devices are 32-bit elements; how exact they have to be, the bound alone decides.
A program may use at most 128 MiB of HBM per device.

v0:
```python
import jax
import jax.numpy as jnp
from jax import lax
from jax.sharding import Mesh
from jax.sharding import PartitionSpec as P

ITERS = 5
GX = ("gx_0", "gx_1")
GY = ("gy_0", "gy_1")
GX_GY_GZ = ("gx_0", "gx_1", "gy_0", "gy_1", "gz")


centre = 7.25
half_width = 6.75


def padded(cells, sides, width, closed):
    for axis, dim in sides:
        count = lax.axis_size(axis)
        ends = count if closed else count - 1
        head = lax.slice_in_dim(cells, 0, width, axis=dim)
        tail = lax.slice_in_dim(cells, cells.shape[dim] - width, cells.shape[dim], axis=dim)
        cells = jnp.concatenate(
            [
                lax.ppermute(tail, axis, [(i, (i + 1) % count) for i in range(ends)]),
                cells,
                lax.ppermute(head, axis, [((i + 1) % count, i) for i in range(ends)]),
            ],
            axis=dim,
        )
    return cells


def one_axis_at_a_time(shard, axes):
    for axis in axes:
        shard = lax.psum(shard, axis)
    return shard


def chebyshev_weights(count):
    ratio_value = centre / half_width
    weights = [1.0 / ratio_value]
    for iteration in range(count):
        weights.append(1.0 / (2.0 * ratio_value - weights[-1]))
    return weights


def combine(middle, plus_x, minus_x, plus_y, minus_y, plus_z, minus_z, reaction, velocity):
    beside = (1.0 - velocity[0]) * plus_x + (1.0 + velocity[0]) * minus_x
    beside = beside + (1.0 - velocity[1]) * plus_y + (1.0 + velocity[1]) * minus_y
    beside = beside + (1.0 - velocity[2]) * plus_z + (1.0 + velocity[2]) * minus_z
    return (6.0 + reaction) * middle - beside


def apply_single(values, reaction, velocity):
    wrapped = padded(values, ((GX, 0),), 1, True)
    opened = padded(values, ((GY, 1), ("gz", 2)), 1, False)
    return combine(
        values,
        wrapped[2:],
        wrapped[:-2],
        opened[:, 2:, 1:-1],
        opened[:, :-2, 1:-1],
        opened[:, 1:-1, 2:],
        opened[:, 1:-1, :-2],
        reaction,
        velocity,
    )


def local(right_side, reaction, velocity):
    weights = chebyshev_weights(ITERS)
    solution = jnp.zeros_like(right_side)
    residual = right_side
    direction = right_side / centre
    for iteration in range(ITERS):
        applied = apply_single(direction, reaction, velocity)
        solution = solution + direction
        residual = residual - applied
        if iteration + 1 < ITERS:
            direction = (
                weights[iteration + 1] * weights[iteration] * direction
                + 2.0 * weights[iteration + 1] / half_width * residual
            )
    local_sum = jnp.sum(residual * residual)
    total = one_axis_at_a_time(local_sum, GX_GY_GZ)
    cells_all = (
        residual.shape[0]
        * residual.shape[1]
        * residual.shape[2]
        * lax.axis_size(GX)
        * lax.axis_size(GY)
        * lax.axis_size("gz")
    )
    residual_norm = jnp.sqrt(total / cells_all + 1e-06)
    return (solution, residual, residual_norm)


def solution(mesh):
    finer = Mesh(
        mesh.devices.reshape(4, 4, 2, 2, mesh.shape["gz"]), ("gx_0", "gx_1", "gy_0", "gy_1", "gz")
    )
    return jax.shard_map(
        local,
        mesh=finer,
        in_specs=(P(GX, GY, "gz"), P(GX, GY, "gz"), P(None, GX, GY, "gz")),
        out_specs=(P(GX, GY, "gz"), P(GX, GY, "gz"), P()),
        check_vma=False,
    )
```

profile of v0, /device:TPU:1, one launch (start us, length us, event | category | flops | bytes accessed | tf_op | source)
XLA Modules:
  0.0 212.4 jit_solution(18094111306749778355)
XLA Ops:
  0.6 1.8 broadcast_multiply_fusion
  2.6 3.3 %collective-permute-start.2 = (f32[16,1,512]{2,0,1:T(8,128)S(1)}, f32[16,1,512]{2,0,1:T(8,128)S(1)}, u32[]{:S(2)}, u32[]{:S(2)}) collective-permute-start(f32[16,1,512]{2,0,1:T(8,128)S(1)} %copy.15), channel_id=1, source_target_pairs={{2,0},{4,2},{6,4},{3,1},{5,3},{7,5},{10,8},{12,10},{14,12},{11,9},... | collective-permute-start | bytes 98312 | tf_op jit(solution)/shard_map/ppermute | solution.py:27
  5.9 5.5 %collective-permute-start.3 = (f32[16,1,512]{2,0,1:T(8,128)S(1)}, f32[16,1,512]{2,0,1:T(8,128)S(1)}, u32[]{:S(2)}, u32[]{:S(2)}) collective-permute-start(f32[16,1,512]{2,0,1:T(8,128)S(1)} %copy.17), channel_id=1, source_target_pairs={{0,2},{2,4},{4,6},{1,3},{3,5},{5,7},{8,10},{10,12},{12,14},{9,11},... | collective-permute-start | bytes 98312 | tf_op jit(solution)/shard_map/ppermute | solution.py:25
  12.1 4.9 %collective-permute-start = (f32[1,64,512]{2,1,0:T(8,128)}, f32[1,64,512]{2,1,0:T(8,128)S(1)}, u32[]{:S(2)}, u32[]{:S(2)}) collective-permute-start(f32[1,64,512]{2,1,0:T(8,128)} %get-tuple-element.42), channel_id=1, source_target_pairs={{8,0},{16,8},{24,16},{32,24},{40,32},{48,40},{56,48},{64,56},{72,6... | collective-permute-start | bytes 393224 | tf_op jit(solution)/shard_map/ppermute | solution.py:27
  19.3 4.0 %collective-permute-start.5 = (f32[16,66,1]{1,0,2:T(8,128)S(1)}, f32[16,66,1]{1,0,2:T(8,128)S(1)}, u32[]{:S(2)}, u32[]{:S(2)}) collective-permute-start(f32[16,66,1]{1,0,2:T(8,128)S(1)} %copy.23), channel_id=1, source_target_pairs={{0,1},{2,3},{4,5},{6,7},{8,9},{10,11},{12,13},{14,15},{16,17},{18,... | collective-permute-start | bytes 12680 | tf_op jit(solution)/shard_map/ppermute | solution.py:25
  24.5 13.1 %multiply_add_fusion.3 = (f32[16,64,512]{2,1,0:T(8,128)S(1)}, f32[16,64,512]{2,1,0:T(8,128)}) fusion(f32[16,64,512]{2,1,0:T(8,128)} %param.3, f32[16,1,512]{2,1,0:T(1,128)S(1)} %copy.16, f32[16,64,512]{2,1,0:T(8,128)} %copy-done.5, f32[16,1,512]{2,1,0:T(1,128)S(1)} %copy.18, f32[16,66,1]{2,1,0:T(8,128)S(1)} %copy.24, f32[16,66,1]{2,1,0:T(8,128)S(1)} %copy.22, ...), kind=kLoop, calls=%fused_computation.120 | loop fusion | flops 17825792 | bytes 17113344 | tf_op jit(solution)/shard_map/add | solution.py:82
  37.7 1.9 collective-permute-start.8
  39.6 5.1 %collective-permute-start.9 = (f32[16,1,512]{2,0,1:T(8,128)S(1)}, f32[16,1,512]{2,0,1:T(8,128)S(1)}, u32[]{:S(2)}, u32[]{:S(2)}) collective-permute-start(f32[16,1,512]{2,0,1:T(8,128)S(1)} %copy.27), channel_id=1, source_target_pairs={{0,2},{2,4},{4,6},{1,3},{3,5},{5,7},{8,10},{10,12},{12,14},{9,11},... | collective-permute-start | bytes 98312 | tf_op jit(solution)/shard_map/ppermute | solution.py:25
  45.5 4.8 %collective-permute-start.6 = (f32[1,64,512]{2,1,0:T(8,128)}, f32[1,64,512]{2,1,0:T(8,128)S(1)}, u32[]{:S(2)}, u32[]{:S(2)}) collective-permute-start(f32[1,64,512]{2,1,0:T(8,128)} %get-tuple-element.38), channel_id=1, source_target_pairs={{8,0},{16,8},{24,16},{32,24},{40,32},{48,40},{56,48},{64,56},{72,6... | collective-permute-start | bytes 393224 | tf_op jit(solution)/shard_map/ppermute | solution.py:27
  52.5 4.0 %collective-permute-start.11 = (f32[16,66,1]{1,0,2:T(8,128)S(1)}, f32[16,66,1]{1,0,2:T(8,128)S(1)}, u32[]{:S(2)}, u32[]{:S(2)}) collective-permute-start(f32[16,66,1]{1,0,2:T(8,128)S(1)} %copy.33), channel_id=1, source_target_pairs={{0,1},{2,3},{4,5},{6,7},{8,9},{10,11},{12,13},{14,15},{16,17},{18,... | collective-permute-start | bytes 12680 | tf_op jit(solution)/shard_map/ppermute | solution.py:25
  57.7 13.0 %multiply_add_fusion.2 = (f32[16,64,512]{2,1,0:T(8,128)S(1)}, f32[16,64,512]{2,1,0:T(8,128)}) fusion(f32[16,64,512]{2,1,0:T(8,128)} %copy-done.1, f32[16,64,512]{2,1,0:T(8,128)} %get-tuple-element.15, f32[16,1,512]{2,1,0:T(1,128)S(1)} %copy.26, f32[16,1,512]{2,1,0:T(1,128)S(1)} %copy.28, f32[16,66,1]{2,1,0:T(8,128)S(1)} %copy.34, ...), kind=kLoop, calls=%fused_computation.119 | loop fusion | flops 17825792 | bytes 17113344 | tf_op jit(solution)/shard_map/add | solution.py:82
  70.8 1.9 collective-permute-start.14
  72.7 5.1 %collective-permute-start.15 = (f32[16,1,512]{2,0,1:T(8,128)S(1)}, f32[16,1,512]{2,0,1:T(8,128)S(1)}, u32[]{:S(2)}, u32[]{:S(2)}) collective-permute-start(f32[16,1,512]{2,0,1:T(8,128)S(1)} %copy.37), channel_id=1, source_target_pairs={{0,2},{2,4},{4,6},{1,3},{3,5},{5,7},{8,10},{10,12},{12,14},{9,11},... | collective-permute-start | bytes 98312 | tf_op jit(solution)/shard_map/ppermute | solution.py:25
  78.6 4.6 %collective-permute-start.12 = (f32[1,64,512]{2,1,0:T(8,128)}, f32[1,64,512]{2,1,0:T(8,128)S(1)}, u32[]{:S(2)}, u32[]{:S(2)}) collective-permute-start(f32[1,64,512]{2,1,0:T(8,128)} %get-tuple-element.34), channel_id=1, source_target_pairs={{8,0},{16,8},{24,16},{32,24},{40,32},{48,40},{56,48},{64,56},{72,6... | collective-permute-start | bytes 393224 | tf_op jit(solution)/shard_map/ppermute | solution.py:27
  85.4 4.2 %collective-permute-start.17 = (f32[16,66,1]{1,0,2:T(8,128)S(1)}, f32[16,66,1]{1,0,2:T(8,128)S(1)}, u32[]{:S(2)}, u32[]{:S(2)}) collective-permute-start(f32[16,66,1]{1,0,2:T(8,128)S(1)} %copy.43), channel_id=1, source_target_pairs={{0,1},{2,3},{4,5},{6,7},{8,9},{10,11},{12,13},{14,15},{16,17},{18,... | collective-permute-start | bytes 12680 | tf_op jit(solution)/shard_map/ppermute | solution.py:25
  90.7 12.1 %multiply_add_fusion.1 = (f32[16,64,512]{2,1,0:T(8,128)S(1)}, f32[16,64,512]{2,1,0:T(8,128)}) fusion(f32[16,64,512]{2,1,0:T(8,128)} %copy-done.2, f32[16,64,512]{2,1,0:T(8,128)} %get-tuple-element.13, f32[16,1,512]{2,1,0:T(1,128)S(1)} %copy.36, f32[16,1,512]{2,1,0:T(1,128)S(1)} %copy.38, f32[16,66,1]{2,1,0:T(8,128)S(1)} %copy.44, ...), kind=kLoop, calls=%fused_computation.118 | loop fusion | flops 17825792 | bytes 17113344 | tf_op jit(solution)/shard_map/add | solution.py:82
  102.9 1.9 collective-permute-start.20
  104.8 5.1 %collective-permute-start.21 = (f32[16,1,512]{2,0,1:T(8,128)S(1)}, f32[16,1,512]{2,0,1:T(8,128)S(1)}, u32[]{:S(2)}, u32[]{:S(2)}) collective-permute-start(f32[16,1,512]{2,0,1:T(8,128)S(1)} %copy.47), channel_id=1, source_target_pairs={{0,2},{2,4},{4,6},{1,3},{3,5},{5,7},{8,10},{10,12},{12,14},{9,11},... | collective-permute-start | bytes 98312 | tf_op jit(solution)/shard_map/ppermute | solution.py:25
  110.7 4.6 %collective-permute-start.18 = (f32[1,64,512]{2,1,0:T(8,128)}, f32[1,64,512]{2,1,0:T(8,128)S(1)}, u32[]{:S(2)}, u32[]{:S(2)}) collective-permute-start(f32[1,64,512]{2,1,0:T(8,128)} %get-tuple-element.30), channel_id=1, source_target_pairs={{8,0},{16,8},{24,16},{32,24},{40,32},{48,40},{56,48},{64,56},{72,6... | collective-permute-start | bytes 393224 | tf_op jit(solution)/shard_map/ppermute | solution.py:27
  117.5 4.0 %collective-permute-start.23 = (f32[16,66,1]{1,0,2:T(8,128)S(1)}, f32[16,66,1]{1,0,2:T(8,128)S(1)}, u32[]{:S(2)}, u32[]{:S(2)}) collective-permute-start(f32[16,66,1]{1,0,2:T(8,128)S(1)} %copy.53), channel_id=1, source_target_pairs={{0,1},{2,3},{4,5},{6,7},{8,9},{10,11},{12,13},{14,15},{16,17},{18,... | collective-permute-start | bytes 12680 | tf_op jit(solution)/shard_map/ppermute | solution.py:25
  122.8 12.6 %multiply_add_fusion = (f32[16,64,512]{2,1,0:T(8,128)S(1)}, f32[16,64,512]{2,1,0:T(8,128)}) fusion(f32[16,64,512]{2,1,0:T(8,128)} %copy-done.3, f32[16,64,512]{2,1,0:T(8,128)} %get-tuple-element.11, f32[16,1,512]{2,1,0:T(1,128)S(1)} %copy.46, f32[16,1,512]{2,1,0:T(1,128)S(1)} %copy.48, f32[16,66,1]{2,1,0:T(8,128)S(1)} %copy.54, f32[16,66,1]{2,1,0:T(8,128)S(1)} %copy.52, ...), kind=kLoop, calls=%fused_computation.116 | loop fusion | flops 17825792 | bytes 17113344 | tf_op jit(solution)/shard_map/add | solution.py:82
  135.5 1.9 collective-permute-start.26
  137.4 5.1 %collective-permute-start.27 = (f32[16,1,512]{2,0,1:T(8,128)S(1)}, f32[16,1,512]{2,0,1:T(8,128)S(1)}, u32[]{:S(2)}, u32[]{:S(2)}) collective-permute-start(f32[16,1,512]{2,0,1:T(8,128)S(1)} %copy.57), channel_id=1, source_target_pairs={{0,2},{2,4},{4,6},{1,3},{3,5},{5,7},{8,10},{10,12},{12,14},{9,11},... | collective-permute-start | bytes 98312 | tf_op jit(solution)/shard_map/ppermute | solution.py:25
  143.3 4.6 %collective-permute-start.24 = (f32[1,64,512]{2,1,0:T(8,128)}, f32[1,64,512]{2,1,0:T(8,128)S(1)}, u32[]{:S(2)}, u32[]{:S(2)}) collective-permute-start(f32[1,64,512]{2,1,0:T(8,128)} %get-tuple-element.26), channel_id=1, source_target_pairs={{8,0},{16,8},{24,16},{32,24},{40,32},{48,40},{56,48},{64,56},{72,6... | collective-permute-start | bytes 393224 | tf_op jit(solution)/shard_map/ppermute | solution.py:27
  150.1 4.0 %collective-permute-start.29 = (f32[16,66,1]{1,0,2:T(8,128)S(1)}, f32[16,66,1]{1,0,2:T(8,128)S(1)}, u32[]{:S(2)}, u32[]{:S(2)}) collective-permute-start(f32[16,66,1]{1,0,2:T(8,128)S(1)} %copy.63), channel_id=1, source_target_pairs={{0,1},{2,3},{4,5},{6,7},{8,9},{10,11},{12,13},{14,15},{16,17},{18,... | collective-permute-start | bytes 12680 | tf_op jit(solution)/shard_map/ppermute | solution.py:25
  155.3 12.7 %multiply_reduce_fusion = (f32[]{:T(128)}, f32[16,64,512]{2,1,0:T(8,128)}) fusion(f32[16,64,512]{2,1,0:T(8,128)} %get-tuple-element.9, f32[16,1,512]{2,1,0:T(1,128)S(1)} %copy.56, f32[16,64,512]{2,1,0:T(8,128)} %copy-done.4, f32[16,1,512]{2,1,0:T(1,128)S(1)} %copy.58, f32[16,66,1]{2,1,0:T(8,128)S(1)} %copy.64, f32[16,66,1]{2,1,0:T(8,128)S(1)} %copy.62, ...), kind=kLoop, calls=%fused_computation.115 | loop fusion | flops 17301504 | bytes 15016196 | tf_op jit(solution)/shard_map/reduce_sum | solution.py:85
  168.0 6.6 %psum.35 = f32[]{:T(128)} all-reduce(f32[]{:T(128)} %get-tuple-element.6), channel_id=1, replica_groups=mesh['gx_0'=4,'gx_1'=4,'gy_0'=2,'gy_1'=2,'gz'=2] {'gx_0'}, use_global_device_ids=true, to_apply=%region_1.0 | all-reduce | flops 1 | bytes 8 | tf_op jit(solution)/shard_map/psum | solution.py:36
  174.6 11.4 %psum.36 = f32[]{:T(128)} all-reduce(f32[]{:T(128)} %psum.35), channel_id=1, replica_groups=mesh['gx_0'=4,'gx_1'=4,'gy_0'=2,'gy_1'=2,'gz'=2] {'gx_1'}, use_global_device_ids=true, to_apply=%region_2.0 | all-reduce | flops 1 | bytes 8 | tf_op jit(solution)/shard_map/psum | solution.py:36
  186.1 5.9 %psum.37 = f32[]{:T(128)} all-reduce(f32[]{:T(128)} %psum.36), channel_id=1, replica_groups=mesh['gx_0'=4,'gx_1'=4,'gy_0'=2,'gy_1'=2,'gz'=2] {'gy_0'}, use_global_device_ids=true, to_apply=%region_3.0 | all-reduce | flops 1 | bytes 8 | tf_op jit(solution)/shard_map/psum | solution.py:36
  192.0 6.9 %psum.38 = f32[]{:T(128)} all-reduce(f32[]{:T(128)} %psum.37), channel_id=1, replica_groups=mesh['gx_0'=4,'gx_1'=4,'gy_0'=2,'gy_1'=2,'gz'=2] {'gy_1'}, use_global_device_ids=true, to_apply=%region_4.0 | all-reduce | flops 1 | bytes 8 | tf_op jit(solution)/shard_map/psum | solution.py:36
  198.9 6.8 %add_add_fusion = f32[16,64,512]{2,1,0:T(8,128)} fusion(f32[16,64,512]{2,1,0:T(8,128)} %copy-done.3, f32[16,64,512]{2,1,0:T(8,128)} %copy-done.2, f32[16,64,512]{2,1,0:T(8,128)} %copy-done.1, f32[16,64,512]{2,1,0:T(8,128)} %get-tuple-element.9, f32[16,64,512]{2,1,0:T(8,128)} %param.3), kind=kLoop, calls=%fused_computation.117 | loop fusion | flops 4194304 | bytes 12582912 | tf_op jit(solution)/shard_map/add | solution.py:78
  205.7 4.9 %psum.39 = f32[]{:T(128)} all-reduce(f32[]{:T(128)} %psum.38), channel_id=1, replica_groups=mesh['gx_0'=4,'gx_1'=4,'gy_0'=2,'gy_1'=2,'gz'=2] {'gz'}, use_global_device_ids=true, to_apply=%region_5.0 | all-reduce | flops 1 | bytes 8 | tf_op jit(solution)/shard_map/psum | solution.py:36
  (107 shorter events, 20.8 us)
Async XLA Ops:
  2.5 14.9 %copy-start.5 = (f32[16,64,512]{2,1,0:T(8,128)}, f32[16,64,512]{2,1,0:T(8,128)S(1)}, u32[]{:S(2)}) copy-start(f32[16,64,512]{2,1,0:T(8,128)S(1)} %broadcast_multiply_fusion) | copy-start | bytes 6291460
  2.6 14.5 %collective-permute-start.2 = (f32[16,1,512]{2,0,1:T(8,128)S(1)}, f32[16,1,512]{2,0,1:T(8,128)S(1)}, u32[]{:S(2)}, u32[]{:S(2)}) collective-permute-start(f32[16,1,512]{2,0,1:T(8,128)S(1)} %copy.15), channel_id=1, source_target_pairs={{2,0},{4,2},{6,4},{3,1},{5,3},{7,5},{10,8},{12,10},{14,12},{11,9},... | collective-permute-start | bytes 98312 | tf_op jit(solution)/shard_map/ppermute | solution.py:27
  5.9 11.2 %collective-permute-start.3 = (f32[16,1,512]{2,0,1:T(8,128)S(1)}, f32[16,1,512]{2,0,1:T(8,128)S(1)}, u32[]{:S(2)}, u32[]{:S(2)}) collective-permute-start(f32[16,1,512]{2,0,1:T(8,128)S(1)} %copy.17), channel_id=1, source_target_pairs={{0,2},{2,4},{4,6},{1,3},{3,5},{5,7},{8,10},{10,12},{12,14},{9,11},... | collective-permute-start | bytes 98312 | tf_op jit(solution)/shard_map/ppermute | solution.py:25
  12.1 12.3 %collective-permute-start = (f32[1,64,512]{2,1,0:T(8,128)}, f32[1,64,512]{2,1,0:T(8,128)S(1)}, u32[]{:S(2)}, u32[]{:S(2)}) collective-permute-start(f32[1,64,512]{2,1,0:T(8,128)} %get-tuple-element.42), channel_id=1, source_target_pairs={{8,0},{16,8},{24,16},{32,24},{40,32},{48,40},{56,48},{64,56},{72,6... | collective-permute-start | bytes 393224 | tf_op jit(solution)/shard_map/ppermute | solution.py:27
  17.0 7.5 %collective-permute-start.1 = (f32[1,64,512]{2,1,0:T(8,128)}, f32[1,64,512]{2,1,0:T(8,128)}, u32[]{:S(2)}, u32[]{:S(2)}) collective-permute-start(f32[1,64,512]{2,1,0:T(8,128)} %get-tuple-element.43), channel_id=1, source_target_pairs={{0,8},{8,16},{16,24},{24,32},{32,40},{40,48},{48,56},{56,64},{64,7... | collective-permute-start | bytes 393224 | tf_op jit(solution)/shard_map/ppermute | solution.py:25
  17.7 5.7 %collective-permute-start.4 = (f32[16,66,1]{1,0,2:T(8,128)S(1)}, f32[16,66,1]{1,0,2:T(8,128)S(1)}, u32[]{:S(2)}, u32[]{:S(2)}) collective-permute-start(f32[16,66,1]{1,0,2:T(8,128)S(1)} %copy.21), channel_id=1, source_target_pairs={{1,0},{3,2},{5,4},{7,6},{9,8},{11,10},{13,12},{15,14},{17,16},{19,... | collective-permute-start | bytes 12680 | tf_op jit(solution)/shard_map/ppermute | solution.py:27
  19.3 4.8 %collective-permute-start.5 = (f32[16,66,1]{1,0,2:T(8,128)S(1)}, f32[16,66,1]{1,0,2:T(8,128)S(1)}, u32[]{:S(2)}, u32[]{:S(2)}) collective-permute-start(f32[16,66,1]{1,0,2:T(8,128)S(1)} %copy.23), channel_id=1, source_target_pairs={{0,1},{2,3},{4,5},{6,7},{8,9},{10,11},{12,13},{14,15},{16,17},{18,... | collective-permute-start | bytes 12680 | tf_op jit(solution)/shard_map/ppermute | solution.py:25
  37.6 13.0 %copy-start.1 = (f32[16,64,512]{2,1,0:T(8,128)}, f32[16,64,512]{2,1,0:T(8,128)S(1)}, u32[]{:S(2)}) copy-start(f32[16,64,512]{2,1,0:T(8,128)S(1)} %get-tuple-element.14) | copy-start | bytes 6291460
  37.7 12.6 %collective-permute-start.8 = (f32[16,1,512]{2,0,1:T(8,128)S(1)}, f32[16,1,512]{2,0,1:T(8,128)S(1)}, u32[]{:S(2)}, u32[]{:S(2)}) collective-permute-start(f32[16,1,512]{2,0,1:T(8,128)S(1)} %copy.25), channel_id=1, source_target_pairs={{2,0},{4,2},{6,4},{3,1},{5,3},{7,5},{10,8},{12,10},{14,12},{11,9},... | collective-permute-start | bytes 98312 | tf_op jit(solution)/shard_map/ppermute | solution.py:27
  39.6 10.7 %collective-permute-start.9 = (f32[16,1,512]{2,0,1:T(8,128)S(1)}, f32[16,1,512]{2,0,1:T(8,128)S(1)}, u32[]{:S(2)}, u32[]{:S(2)}) collective-permute-start(f32[16,1,512]{2,0,1:T(8,128)S(1)} %copy.27), channel_id=1, source_target_pairs={{0,2},{2,4},{4,6},{1,3},{3,5},{5,7},{8,10},{10,12},{12,14},{9,11},... | collective-permute-start | bytes 98312 | tf_op jit(solution)/shard_map/ppermute | solution.py:25
  45.5 12.0 %collective-permute-start.6 = (f32[1,64,512]{2,1,0:T(8,128)}, f32[1,64,512]{2,1,0:T(8,128)S(1)}, u32[]{:S(2)}, u32[]{:S(2)}) collective-permute-start(f32[1,64,512]{2,1,0:T(8,128)} %get-tuple-element.38), channel_id=1, source_target_pairs={{8,0},{16,8},{24,16},{32,24},{40,32},{48,40},{56,48},{64,56},{72,6... | collective-permute-start | bytes 393224 | tf_op jit(solution)/shard_map/ppermute | solution.py:27
  50.3 7.5 %collective-permute-start.7 = (f32[1,64,512]{2,1,0:T(8,128)}, f32[1,64,512]{2,1,0:T(8,128)}, u32[]{:S(2)}, u32[]{:S(2)}) collective-permute-start(f32[1,64,512]{2,1,0:T(8,128)} %get-tuple-element.39), channel_id=1, source_target_pairs={{0,8},{8,16},{16,24},{24,32},{32,40},{40,48},{48,56},{56,64},{64,7... | collective-permute-start | bytes 393224 | tf_op jit(solution)/shard_map/ppermute | solution.py:25
  50.9 5.5 %collective-permute-start.10 = (f32[16,66,1]{1,0,2:T(8,128)S(1)}, f32[16,66,1]{1,0,2:T(8,128)S(1)}, u32[]{:S(2)}, u32[]{:S(2)}) collective-permute-start(f32[16,66,1]{1,0,2:T(8,128)S(1)} %copy.31), channel_id=1, source_target_pairs={{1,0},{3,2},{5,4},{7,6},{9,8},{11,10},{13,12},{15,14},{17,16},{19,... | collective-permute-start | bytes 12680 | tf_op jit(solution)/shard_map/ppermute | solution.py:27
  52.5 4.8 %collective-permute-start.11 = (f32[16,66,1]{1,0,2:T(8,128)S(1)}, f32[16,66,1]{1,0,2:T(8,128)S(1)}, u32[]{:S(2)}, u32[]{:S(2)}) collective-permute-start(f32[16,66,1]{1,0,2:T(8,128)S(1)} %copy.33), channel_id=1, source_target_pairs={{0,1},{2,3},{4,5},{6,7},{8,9},{10,11},{12,13},{14,15},{16,17},{18,... | collective-permute-start | bytes 12680 | tf_op jit(solution)/shard_map/ppermute | solution.py:25
  70.8 12.4 %collective-permute-start.14 = (f32[16,1,512]{2,0,1:T(8,128)S(1)}, f32[16,1,512]{2,0,1:T(8,128)S(1)}, u32[]{:S(2)}, u32[]{:S(2)}) collective-permute-start(f32[16,1,512]{2,0,1:T(8,128)S(1)} %copy.35), channel_id=1, source_target_pairs={{2,0},{4,2},{6,4},{3,1},{5,3},{7,5},{10,8},{12,10},{14,12},{11,9},... | collective-permute-start | bytes 98312 | tf_op jit(solution)/shard_map/ppermute | solution.py:27
  72.7 10.5 %collective-permute-start.15 = (f32[16,1,512]{2,0,1:T(8,128)S(1)}, f32[16,1,512]{2,0,1:T(8,128)S(1)}, u32[]{:S(2)}, u32[]{:S(2)}) collective-permute-start(f32[16,1,512]{2,0,1:T(8,128)S(1)} %copy.37), channel_id=1, source_target_pairs={{0,2},{2,4},{4,6},{1,3},{3,5},{5,7},{8,10},{10,12},{12,14},{9,11},... | collective-permute-start | bytes 98312 | tf_op jit(solution)/shard_map/ppermute | solution.py:25
  78.6 11.9 %collective-permute-start.12 = (f32[1,64,512]{2,1,0:T(8,128)}, f32[1,64,512]{2,1,0:T(8,128)S(1)}, u32[]{:S(2)}, u32[]{:S(2)}) collective-permute-start(f32[1,64,512]{2,1,0:T(8,128)} %get-tuple-element.34), channel_id=1, source_target_pairs={{8,0},{16,8},{24,16},{32,24},{40,32},{48,40},{56,48},{64,56},{72,6... | collective-permute-start | bytes 393224 | tf_op jit(solution)/shard_map/ppermute | solution.py:27
  83.2 7.5 %collective-permute-start.13 = (f32[1,64,512]{2,1,0:T(8,128)}, f32[1,64,512]{2,1,0:T(8,128)}, u32[]{:S(2)}, u32[]{:S(2)}) collective-permute-start(f32[1,64,512]{2,1,0:T(8,128)} %get-tuple-element.35), channel_id=1, source_target_pairs={{0,8},{8,16},{16,24},{24,32},{32,40},{40,48},{48,56},{56,64},{64,7... | collective-permute-start | bytes 393224 | tf_op jit(solution)/shard_map/ppermute | solution.py:25
  83.9 5.7 %collective-permute-start.16 = (f32[16,66,1]{1,0,2:T(8,128)S(1)}, f32[16,66,1]{1,0,2:T(8,128)S(1)}, u32[]{:S(2)}, u32[]{:S(2)}) collective-permute-start(f32[16,66,1]{1,0,2:T(8,128)S(1)} %copy.41), channel_id=1, source_target_pairs={{1,0},{3,2},{5,4},{7,6},{9,8},{11,10},{13,12},{15,14},{17,16},{19,... | collective-permute-start | bytes 12680 | tf_op jit(solution)/shard_map/ppermute | solution.py:27
  85.4 4.8 %collective-permute-start.17 = (f32[16,66,1]{1,0,2:T(8,128)S(1)}, f32[16,66,1]{1,0,2:T(8,128)S(1)}, u32[]{:S(2)}, u32[]{:S(2)}) collective-permute-start(f32[16,66,1]{1,0,2:T(8,128)S(1)} %copy.43), channel_id=1, source_target_pairs={{0,1},{2,3},{4,5},{6,7},{8,9},{10,11},{12,13},{14,15},{16,17},{18,... | collective-permute-start | bytes 12680 | tf_op jit(solution)/shard_map/ppermute | solution.py:25
  102.9 12.5 %collective-permute-start.20 = (f32[16,1,512]{2,0,1:T(8,128)S(1)}, f32[16,1,512]{2,0,1:T(8,128)S(1)}, u32[]{:S(2)}, u32[]{:S(2)}) collective-permute-start(f32[16,1,512]{2,0,1:T(8,128)S(1)} %copy.45), channel_id=1, source_target_pairs={{2,0},{4,2},{6,4},{3,1},{5,3},{7,5},{10,8},{12,10},{14,12},{11,9},... | collective-permute-start | bytes 98312 | tf_op jit(solution)/shard_map/ppermute | solution.py:27
  104.8 10.6 %collective-permute-start.21 = (f32[16,1,512]{2,0,1:T(8,128)S(1)}, f32[16,1,512]{2,0,1:T(8,128)S(1)}, u32[]{:S(2)}, u32[]{:S(2)}) collective-permute-start(f32[16,1,512]{2,0,1:T(8,128)S(1)} %copy.47), channel_id=1, source_target_pairs={{0,2},{2,4},{4,6},{1,3},{3,5},{5,7},{8,10},{10,12},{12,14},{9,11},... | collective-permute-start | bytes 98312 | tf_op jit(solution)/shard_map/ppermute | solution.py:25
  110.7 11.9 %collective-permute-start.18 = (f32[1,64,512]{2,1,0:T(8,128)}, f32[1,64,512]{2,1,0:T(8,128)S(1)}, u32[]{:S(2)}, u32[]{:S(2)}) collective-permute-start(f32[1,64,512]{2,1,0:T(8,128)} %get-tuple-element.30), channel_id=1, source_target_pairs={{8,0},{16,8},{24,16},{32,24},{40,32},{48,40},{56,48},{64,56},{72,6... | collective-permute-start | bytes 393224 | tf_op jit(solution)/shard_map/ppermute | solution.py:27
  115.3 7.5 %collective-permute-start.19 = (f32[1,64,512]{2,1,0:T(8,128)}, f32[1,64,512]{2,1,0:T(8,128)}, u32[]{:S(2)}, u32[]{:S(2)}) collective-permute-start(f32[1,64,512]{2,1,0:T(8,128)} %get-tuple-element.31), channel_id=1, source_target_pairs={{0,8},{8,16},{16,24},{24,32},{32,40},{40,48},{48,56},{56,64},{64,7... | collective-permute-start | bytes 393224 | tf_op jit(solution)/shard_map/ppermute | solution.py:25
  116.0 5.5 %collective-permute-start.22 = (f32[16,66,1]{1,0,2:T(8,128)S(1)}, f32[16,66,1]{1,0,2:T(8,128)S(1)}, u32[]{:S(2)}, u32[]{:S(2)}) collective-permute-start(f32[16,66,1]{1,0,2:T(8,128)S(1)} %copy.51), channel_id=1, source_target_pairs={{1,0},{3,2},{5,4},{7,6},{9,8},{11,10},{13,12},{15,14},{17,16},{19,... | collective-permute-start | bytes 12680 | tf_op jit(solution)/shard_map/ppermute | solution.py:27
  117.5 4.8 %collective-permute-start.23 = (f32[16,66,1]{1,0,2:T(8,128)S(1)}, f32[16,66,1]{1,0,2:T(8,128)S(1)}, u32[]{:S(2)}, u32[]{:S(2)}) collective-permute-start(f32[16,66,1]{1,0,2:T(8,128)S(1)} %copy.53), channel_id=1, source_target_pairs={{0,1},{2,3},{4,5},{6,7},{8,9},{10,11},{12,13},{14,15},{16,17},{18,... | collective-permute-start | bytes 12680 | tf_op jit(solution)/shard_map/ppermute | solution.py:25
  135.5 12.4 %collective-permute-start.26 = (f32[16,1,512]{2,0,1:T(8,128)S(1)}, f32[16,1,512]{2,0,1:T(8,128)S(1)}, u32[]{:S(2)}, u32[]{:S(2)}) collective-permute-start(f32[16,1,512]{2,0,1:T(8,128)S(1)} %copy.55), channel_id=1, source_target_pairs={{2,0},{4,2},{6,4},{3,1},{5,3},{7,5},{10,8},{12,10},{14,12},{11,9},... | collective-permute-start | bytes 98312 | tf_op jit(solution)/shard_map/ppermute | solution.py:27
  137.4 10.5 %collective-permute-start.27 = (f32[16,1,512]{2,0,1:T(8,128)S(1)}, f32[16,1,512]{2,0,1:T(8,128)S(1)}, u32[]{:S(2)}, u32[]{:S(2)}) collective-permute-start(f32[16,1,512]{2,0,1:T(8,128)S(1)} %copy.57), channel_id=1, source_target_pairs={{0,2},{2,4},{4,6},{1,3},{3,5},{5,7},{8,10},{10,12},{12,14},{9,11},... | collective-permute-start | bytes 98312 | tf_op jit(solution)/shard_map/ppermute | solution.py:25
  143.3 11.9 %collective-permute-start.24 = (f32[1,64,512]{2,1,0:T(8,128)}, f32[1,64,512]{2,1,0:T(8,128)S(1)}, u32[]{:S(2)}, u32[]{:S(2)}) collective-permute-start(f32[1,64,512]{2,1,0:T(8,128)} %get-tuple-element.26), channel_id=1, source_target_pairs={{8,0},{16,8},{24,16},{32,24},{40,32},{48,40},{56,48},{64,56},{72,6... | collective-permute-start | bytes 393224 | tf_op jit(solution)/shard_map/ppermute | solution.py:27
  147.9 7.5 %collective-permute-start.25 = (f32[1,64,512]{2,1,0:T(8,128)}, f32[1,64,512]{2,1,0:T(8,128)}, u32[]{:S(2)}, u32[]{:S(2)}) collective-permute-start(f32[1,64,512]{2,1,0:T(8,128)} %get-tuple-element.27), channel_id=1, source_target_pairs={{0,8},{8,16},{16,24},{24,32},{32,40},{40,48},{48,56},{56,64},{64,7... | collective-permute-start | bytes 393224 | tf_op jit(solution)/shard_map/ppermute | solution.py:25
  148.5 5.5 %collective-permute-start.28 = (f32[16,66,1]{1,0,2:T(8,128)S(1)}, f32[16,66,1]{1,0,2:T(8,128)S(1)}, u32[]{:S(2)}, u32[]{:S(2)}) collective-permute-start(f32[16,66,1]{1,0,2:T(8,128)S(1)} %copy.61), channel_id=1, source_target_pairs={{1,0},{3,2},{5,4},{7,6},{9,8},{11,10},{13,12},{15,14},{17,16},{19,... | collective-permute-start | bytes 12680 | tf_op jit(solution)/shard_map/ppermute | solution.py:27
  150.1 4.8 %collective-permute-start.29 = (f32[16,66,1]{1,0,2:T(8,128)S(1)}, f32[16,66,1]{1,0,2:T(8,128)S(1)}, u32[]{:S(2)}, u32[]{:S(2)}) collective-permute-start(f32[16,66,1]{1,0,2:T(8,128)S(1)} %copy.63), channel_id=1, source_target_pairs={{0,1},{2,3},{4,5},{6,7},{8,9},{10,11},{12,13},{14,15},{16,17},{18,... | collective-permute-start | bytes 12680 | tf_op jit(solution)/shard_map/ppermute | solution.py:25
  (4 other events, 46.0 us)
where the time goes:
time: 213 us; the launch traced here: 212 us
  starting transfers between devices  87.4 us (41%)
  other arithmetic  73.5 us (35%)
  blocking collectives  35.8 us (17%)
  local copies, waits for them, and re-layouts  9.81 us (5%)
  between operations  3.01 us (1%)
  waiting for transfers between devices  2.95 us (1%)
    add x4, other arithmetic, local(): weights[iteration + 1] * weights[iteration] * direction  50.8 us
    ppermute x15, starting transfers between devices, padded(): lax.ppermute(tail, axis, [(i, (i + 1) % count) for i in range(ends)])  46.2 us
    ppermute x15, starting transfers between devices, padded(): lax.ppermute(head, axis, [((i + 1) % count, i) for i in range(ends)])  41.1 us
    psum x5, blocking collectives, one_axis_at_a_time(): shard = lax.psum(shard, axis)  35.8 us
    reduce_sum x1, other arithmetic, local(): local_sum = jnp.sum(residual * residual)  12.7 us
    add x1, other arithmetic, local(): solution = solution + direction  6.79 us
    slice x15, local copies, waits for them, and re-layouts, padded(): head = lax.slice_in_dim(cells, 0, width, axis=dim)  4.85 us
  transfers between devices with their start and end apart: 30, of which 9 were waited for; matrix products, arithmetic and copies ran while one was open for 5% of the time, Pallas kernels for 0%

commit v1 on v0

v1 whole, which is shorter than its diff:
```python
import functools

import jax
import jax.numpy as jnp
from jax import lax
from jax.experimental import pallas as pl
from jax.experimental.pallas import tpu as pltpu
from jax.sharding import PartitionSpec as P

ITERS = 5
centre = 7.25
half_width = 6.75
MESH = pl.DeviceIdType.MESH
F32 = jnp.float32


def chebyshev_weights(count):
    ratio_value = centre / half_width
    weights = [1.0 / ratio_value]
    for iteration in range(count):
        weights.append(1.0 / (2.0 * ratio_value - weights[-1]))
    return weights


NXL, NYL, NT = 16, 64, 4
NJ = NYL // 8
TOP = 8
CELLS = 256 * 256 * 1024


def kernel(
    rhs, rea, vel, sol, res, norm,
    D, V, C, ZS, ZH, G1, G2, G3,
    lf, lr, lc, lv, xs, xr, ys, yr, zs, zr, g1s, g1r, g2s, g2r, g3s, g3r,
):
    gx, gy, gz = lax.axis_index("gx"), lax.axis_index("gy"), lax.axis_index("gz")
    px, py = gx // 4, gx % 4
    yz = gy * 2 + gz
    weights = chebyshev_weights(ITERS)

    def rhs_load(x0, n, t, sem):
        return pltpu.make_async_copy(
            rhs.at[pl.ds(x0, n), :, pl.ds(128 * t, 128)],
            D.at[0, pl.ds(x0 + 1, n), t, pl.ds(TOP, NYL), :],
            sem,
        )

    faces = [rhs_load(x0, 1, t, lf.at[i, t]) for t in range(NT) for i, x0 in enumerate((0, NXL - 1))]
    rest = [rhs_load(1, NXL - 2, t, lr.at[t]) for t in range(NT)]
    coef = [
        pltpu.make_async_copy(rea.at[:, :, pl.ds(128 * t, 128)], C.at[:, t], lc.at[t]) for t in range(NT)
    ] + [
        pltpu.make_async_copy(vel.at[c, :, :, pl.ds(128 * t, 128)], V.at[c, :, t], lv.at[c, t])
        for t in range(NT)
        for c in range(3)
    ]
    for copy in faces + rest + coef:
        copy.start()

    barrier = pltpu.get_barrier_semaphore()
    near = [(gx + 1) % 16, (gx + 15) % 16]
    ring_y = [px * 4 + (py + o) % 4 for o in (1, 2, 3)]
    ring_x = [(gx + 4 * o) % 16 for o in (1, 2, 3)]
    block = [(yz + o) % 8 for o in range(1, 8)]
    peers = [(g, gy, gz) for g in near + ring_y + ring_x] + [(gx, b // 2, b % 2) for b in block]
    for peer in peers:
        pl.semaphore_signal(barrier, inc=1, device_id=peer, device_id_type=MESH)

    zrow = jnp.zeros((1, 128), F32)

    def zero_rows(row):
        def body(x, carry):
            for b in range(2):
                for t in range(NT):
                    D[b, x, t, pl.ds(row, 1), :] = zrow
            return carry

        lax.fori_loop(1, NXL + 1, body, 0)

    @pl.when(gy == 0)
    def _():
        zero_rows(TOP - 1)

    @pl.when(gy == 3)
    def _():
        zero_rows(TOP + NYL)

    for copy in faces:
        copy.wait()
    pl.semaphore_wait(barrier, len(peers))

    x_side = (
        (1, NXL + 1, (gx + 15) % 16),
        (NXL, 0, (gx + 1) % 16),
    )

    def x_copy(buf, side, t):
        src, dst, to = x_side[side]
        return pltpu.make_async_remote_copy(
            src_ref=D.at[buf, src, t, pl.ds(TOP, NYL), :],
            dst_ref=D.at[buf, dst, t, pl.ds(TOP, NYL), :],
            send_sem=xs.at[buf, side, t],
            recv_sem=xr.at[buf, side, t],
            device_id=(to, gy, gz),
            device_id_type=MESH,
        )

    def y_copy(buf, side):
        src = TOP if side == 0 else TOP + NYL - 1
        dst = TOP + NYL if side == 0 else TOP - 1
        to = gy - 1 if side == 0 else gy + 1
        return pltpu.make_async_remote_copy(
            src_ref=D.at[buf, pl.ds(1, NXL), :, pl.ds(src, 1), :],
            dst_ref=D.at[buf, pl.ds(1, NXL), :, pl.ds(dst, 1), :],
            send_sem=ys.at[buf, side],
            recv_sem=yr.at[buf, side],
            device_id=(gx, to, gz),
            device_id_type=MESH,
        )

    def y_each(buf, what):
        if what == "start":
            first, second = gy > 0, gy < 3
        elif what == "recv":
            first, second = gy < 3, gy > 0
        else:
            first, second = gy > 0, gy < 3

        def act(side):
            copy = y_copy(buf, side)
            if what == "start":
                copy.start()
            elif what == "recv":
                copy.wait_recv()
            else:
                copy.wait_send()

        pl.when(first)(lambda: act(0))
        pl.when(second)(lambda: act(1))

    def z_copy(buf):
        return pltpu.make_async_remote_copy(
            src_ref=ZS.at[buf],
            dst_ref=ZH.at[buf],
            send_sem=zs.at[buf],
            recv_sem=zr.at[buf],
            device_id=(gx, gy, 1 - gz),
            device_id_type=MESH,
        )

    lane = lax.broadcasted_iota(jnp.int32, (8, 128), 1)
    first_lane, last_lane = lane == 0, lane == 127
    z_tile = (NT - 1) * (1 - gz)
    low = gz.astype(F32)
    high = 1.0 - low

    def z_pack(buf):
        def body(x, acc):
            for j in range(NJ):
                v = x * NJ + j
                cell = D[buf, x + 1, z_tile, pl.ds(TOP + 8 * j, 8), :]
                cell = pltpu.roll(cell, (v + 1 - gz) % 128, 1)
                acc = jnp.where(lane == v, cell, acc)
            return acc

        ZS[buf] = lax.fori_loop(0, NXL, body, jnp.zeros((8, 128), F32))

    def row_group(step, x, j, tiles, halo, extra=None):
        cur, new = step % 2, (step + 1) % 2
        row = TOP + 8 * j
        lines = pl.ds(8 * j, 8)
        cells, ups, downs = {}, {}, {}

        def cell(t):
            if t not in cells:
                cells[t] = D[cur, x, t, pl.ds(row, 8), :]
            return cells[t]

        def up(t):
            if t not in ups:
                ups[t] = pltpu.roll(cell(t), 127, 1)
            return ups[t]

        def down(t):
            if t not in downs:
                downs[t] = pltpu.roll(cell(t), 1, 1)
            return downs[t]

        if 0 in tiles or NT - 1 in tiles:
            v = (x - 1) * NJ + j
            beyond = pltpu.roll(halo, (127 * (1 - gz) - v + 128) % 128, 1)
        for t in tiles:
            m = cell(t)
            zm = jnp.where(first_lane, down(t - 1) if t else beyond * low, down(t))
            zp = jnp.where(last_lane, up(t + 1) if t < NT - 1 else beyond * high, up(t))
            xm = D[cur, x - 1, t, pl.ds(row, 8), :]
            xp = D[cur, x + 1, t, pl.ds(row, 8), :]
            ym = D[cur, x, t, pl.ds(row - 1, 8), :]
            yp = D[cur, x, t, pl.ds(row + 1, 8), :]
            vx = V[0, x - 1, t, lines, :]
            vy = V[1, x - 1, t, lines, :]
            vz = V[2, x - 1, t, lines, :]
            c = C[x - 1, t, lines, :]
            flow = vx * (xp - xm) + vy * (yp - ym) + vz * (zp - zm)
            beside = ((xp + xm) + (yp + ym)) + (zp + zm)
            applied = (6.0 + c) * m - (beside - flow)
            at = (x - 1, lines, pl.ds(128 * t, 128))
            if step == 0:
                r = m - applied * (1.0 / centre)
                alpha = weights[1] * weights[0] / centre
            else:
                r = res[at] - applied
                alpha = weights[step + 1] * weights[step] if step + 1 < ITERS else 0.0
            res[at] = r
            if step + 1 < ITERS:
                d = alpha * m + (2.0 * weights[step + 1] / half_width) * r
                D[new, x, t, pl.ds(row, 8), :] = d
                if step == 0:
                    sol[at] = m * (1.0 / centre) + d
                else:
                    sol[at] = sol[at] + d
            else:
                extra[(len(extra[-1])) % 4] = extra[len(extra[-1]) % 4] + r * r
                extra[-1].append(0)

    def layers(step, first, last, js, halo):
        def body(x, carry):
            for j in js:
                row_group(step, x, j, range(NT), halo)
            return carry

        lax.fori_loop(first, last, body, 0)

    for t in range(NT):
        for side in range(2):
            x_copy(0, side, t).start()
    for copy in rest:
        copy.wait()
    y_each(0, "start")
    z_pack(0)
    z_copy(0).start()
    for copy in coef:
        copy.wait()

    for step in range(ITERS - 1):
        cur, new = step % 2, (step + 1) % 2
        y_each(cur, "recv")
        z_copy(cur).wait_recv()
        halo = ZH[cur]
        for t in range(NT):
            for side in range(2):
                x_copy(cur, side, t).wait_recv()
            for j in range(NJ):
                for x in (1, NXL):
                    row_group(step, x, j, (t,), halo)
            for side in range(2):
                x_copy(new, side, t).start()
        layers(step, 2, NXL, (0, NJ - 1), halo)
        y_each(new, "start")
        layers(step, 2, NXL, range(1, NJ - 1), halo)
        z_pack(new)
        z_copy(new).start()
        for t in range(NT):
            for side in range(2):
                x_copy(cur, side, t).wait_send()
        y_each(cur, "send")
        z_copy(cur).wait_send()

    step = ITERS - 1
    cur = step % 2
    y_each(cur, "recv")
    z_copy(cur).wait_recv()
    halo = ZH[cur]

    def last_layers(x, sums):
        sums = list(sums) + [[]]
        for j in range(NJ):
            row_group(step, x, j, range(NT), halo, sums)
        return tuple(sums[:4])

    zero = jnp.zeros((8, 128), F32)
    sums = list(lax.fori_loop(2, NXL, last_layers, (zero,) * 4)) + [[]]
    for t in range(NT):
        for side in range(2):
            x_copy(cur, side, t).wait_recv()
        for j in range(NJ):
            for x in (1, NXL):
                row_group(step, x, j, (t,), halo, sums)
    total = (sums[0] + sums[1]) + (sums[2] + sums[3])

    def stage(total, G, send, recv, own, count, place):
        G[own] = total
        copies = [
            pltpu.make_async_remote_copy(
                src_ref=G.at[own],
                dst_ref=G.at[own],
                send_sem=send.at[o - 1],
                recv_sem=recv.at[o - 1],
                device_id=place((own + o) % count),
                device_id_type=MESH,
            )
            for o in range(1, count)
        ]
        for copy in copies:
            copy.start()
        for copy in copies:
            copy.wait_recv()
        total = G[0]
        for i in range(1, count):
            total = total + G[i]
        return total, copies

    total, c1 = stage(total, G1, g1s, g1r, py, 4, lambda p: (px * 4 + p, gy, gz))
    total, c2 = stage(total, G2, g2s, g2r, px, 4, lambda p: (p * 4 + py, gy, gz))
    total, c3 = stage(total, G3, g3s, g3r, yz, 8, lambda p: (gx, p // 2, p % 2))
    whole = jnp.sum(jnp.sum(total, axis=0, keepdims=True), axis=1, keepdims=True)
    norm[...] = jnp.sqrt(whole * (1.0 / CELLS) + 1e-06)
    for t in range(NT):
        for side in range(2):
            x_copy(cur, side, t).wait_send()
    y_each(cur, "send")
    z_copy(cur).wait_send()
    for copy in c1 + c2 + c3:
        copy.wait_send()


def local(right_side, reaction, velocity):
    sem = pltpu.SemaphoreType.DMA
    shape = right_side.shape
    sol, res, norm = pl.pallas_call(
        kernel,
        name="chebyshev",
        out_shape=(pltpu.VMEM(shape, F32), pltpu.VMEM(shape, F32), jax.ShapeDtypeStruct((1, 1), F32)),
        in_specs=[pl.BlockSpec(memory_space=pl.ANY)] * 3,
        out_specs=(pl.BlockSpec(memory_space=pltpu.VMEM),) * 3,
        scratch_shapes=[
            pltpu.VMEM((2, NXL + 2, NT, NYL + 16, 128), F32),
            pltpu.VMEM((3, NXL, NT, NYL, 128), F32),
            pltpu.VMEM((NXL, NT, NYL, 128), F32),
            pltpu.VMEM((2, 8, 128), F32),
            pltpu.VMEM((2, 8, 128), F32),
            pltpu.VMEM((4, 8, 128), F32),
            pltpu.VMEM((4, 8, 128), F32),
            pltpu.VMEM((8, 8, 128), F32),
            sem((2, NT)), sem((NT,)), sem((NT,)), sem((3, NT)),
            sem((2, 2, NT)), sem((2, 2, NT)), sem((2, 2)), sem((2, 2)), sem((2,)), sem((2,)),
            sem((3,)), sem((3,)), sem((3,)), sem((3,)), sem((7,)), sem((7,)),
        ],
        compiler_params=pltpu.CompilerParams(
            collective_id=0, has_side_effects=True, vmem_limit_bytes=24 * 1024 * 1024
        ),
    )(right_side, reaction, velocity)
    return sol, res, norm.reshape(())


def solution(mesh):
    spec = P("gx", "gy", "gz")
    return jax.shard_map(
        local,
        mesh=mesh,
        in_specs=(spec, spec, P(None, "gx", "gy", "gz")),
        out_specs=(spec, spec, P()),
        check_vma=False,
    )
```

time: 213 us -> 89.2 us (0.42)
  starting transfers between devices: 87.4 us -> 0 us
  Pallas kernels: 0 us -> 78 us
  other arithmetic: 73.5 us -> 0 us
  blocking collectives: 35.8 us -> 0 us
  waiting for transfers between devices: 2.95 us -> 0 us
    ppermute x30 -> x0, starting transfers between devices: 87.4 us -> none  [the longest x15 46.2 us: padded(): lax.ppermute(tail, axis, [(i, (i + 1) % count) for i in range(ends)])]
    pallas_call x0 -> x1, Pallas kernels: none -> 78 us  [local(): pl.pallas_call(kernel, name='chebyshev', out_shape=(pltpu.VMEM(shape, F32...]
    add x5 -> x0, other arithmetic: 57.6 us -> none  [the longest x4 50.8 us: local(): weights[iteration + 1] * weights[iteration] * direction]
    psum x5 -> x0, blocking collectives: 35.8 us -> none  [one_axis_at_a_time(): shard = lax.psum(shard, axis)]
    reduce_sum x1 -> x0, other arithmetic: 12.7 us -> none  [local(): local_sum = jnp.sum(residual * residual)]
    unnamed x12 -> x8, local copies, waits for them, and re-layouts: 0.03 us -> 8.6 us
    slice x30 -> x0, local copies, waits for them, and re-layouts: 6.34 us -> none  [the longest x15 4.85 us: padded(): head = lax.slice_in_dim(cells, 0, width, axis=dim)]
    ppermute x20 -> x0, local copies, waits for them, and re-layouts: 3.45 us -> none  [the longest x10 1.72 us: padded(): lax.ppermute(head, axis, [((i + 1) % count, i) for i in range(ends)])]
  transfers between devices with their start and end apart: 30 -> 0, of which waited for: 9 -> 0; matrix products, arithmetic and copies ran while one was open for 5% -> 0% of each run, Pallas kernels for 0% -> 0%
where the time goes in v1:
time: 89.2 us; the launch traced here: 89 us
  Pallas kernels  78 us (87%)
  local copies, waits for them, and re-layouts  8.6 us (10%)
  between operations  2.39 us (3%)
    pallas_call x1, Pallas kernels, local(): pl.pallas_call(kernel, name='chebyshev', out_shape=(pltpu.VMEM(shape, F32...  78 us
    unnamed x8, local copies, waits for them, and re-layouts  8.6 us

profile of v1, /device:TPU:1, one launch (start us, length us, event | category | flops | bytes accessed | tf_op | source)
XLA Modules:
  0.0 89.0 jit_solution(17394920092102434999)
XLA Ops:
  0.6 0.0 copy-start
  0.6 2.8 %copy-done = f32[3,16,64,512]{3,2,1,0:T(8,128)S(1)} copy-done((f32[3,16,64,512]{3,2,1,0:T(8,128)S(1)}, f32[3,16,64,512]{3,2,1,0:T(8,128)}, u32[]{:S(2)}) %copy-start) | copy-done | bytes 6291480
  3.4 0.0 copy-start.1
  3.4 1.6 %copy-done.1 = f32[16,64,512]{2,1,0:T(8,128)S(1)} copy-done((f32[16,64,512]{2,1,0:T(8,128)S(1)}, f32[16,64,512]{2,1,0:T(8,128)}, u32[]{:S(2)}) %copy-start.1) | copy-done | bytes 2097176
  5.0 0.0 copy-start.2
  5.0 1.6 %copy-done.2 = f32[16,64,512]{2,1,0:T(8,128)S(1)} copy-done((f32[16,64,512]{2,1,0:T(8,128)S(1)}, f32[16,64,512]{2,1,0:T(8,128)}, u32[]{:S(2)}) %copy-start.2) | copy-done | bytes 2097176
  6.6 78.0 %chebyshev.1 = (f32[16,64,512]{2,1,0:T(8,128)S(1)}, f32[16,64,512]{2,1,0:T(8,128)S(1)}, f32[1,1]{1,0:T(1,128)}) custom-call(f32[16,64,512]{2,1,0:T(8,128)S(1)} %copy-done.1, f32[16,64,512]{2,1,0:T(8,128)S(1)} %copy-done.2, f32[3,16,64,512]{3,2,1,0:T(8,128)S(1)} %copy-done), custom_call_target="tpu_custom_call" | custom-call | tf_op jit(solution)/shard_map/chebyshev/pallas_call | solution.py:330
  84.6 1.3 %copy.9 = f32[16,64,512]{2,1,0:T(8,128)} copy(f32[16,64,512]{2,1,0:T(8,128)S(1)} %get-tuple-element.9) | data formatting | bytes 4194304
  86.0 1.3 %copy.10 = f32[16,64,512]{2,1,0:T(8,128)} copy(f32[16,64,512]{2,1,0:T(8,128)S(1)} %get-tuple-element.10) | data formatting | bytes 4194304
Async XLA Ops:
  0.6 2.8 %copy-start = (f32[3,16,64,512]{3,2,1,0:T(8,128)S(1)}, f32[3,16,64,512]{3,2,1,0:T(8,128)}, u32[]{:S(2)}) copy-start(f32[3,16,64,512]{3,2,1,0:T(8,128)} %vel.1) | copy-start | bytes 18874372
  3.4 1.6 %copy-start.1 = (f32[16,64,512]{2,1,0:T(8,128)S(1)}, f32[16,64,512]{2,1,0:T(8,128)}, u32[]{:S(2)}) copy-start(f32[16,64,512]{2,1,0:T(8,128)} %rhs.1) | copy-start | bytes 6291460
  5.0 1.6 %copy-start.2 = (f32[16,64,512]{2,1,0:T(8,128)S(1)}, f32[16,64,512]{2,1,0:T(8,128)}, u32[]{:S(2)}) copy-start(f32[16,64,512]{2,1,0:T(8,128)} %rea.1) | copy-start | bytes 6291460

commit v2 on v1

--- a/solution.py
+++ b/solution.py
@@ -331,7 +331,7 @@
         kernel,
         name="chebyshev",
         out_shape=(pltpu.VMEM(shape, F32), pltpu.VMEM(shape, F32), jax.ShapeDtypeStruct((1, 1), F32)),
-        in_specs=[pl.BlockSpec(memory_space=pl.ANY)] * 3,
+        in_specs=[pl.BlockSpec(memory_space=pltpu.HBM)] * 3,
         out_specs=(pl.BlockSpec(memory_space=pltpu.VMEM),) * 3,
         scratch_shapes=[
             pltpu.VMEM((2, NXL + 2, NT, NYL + 16, 128), F32),
@@ -349,7 +349,7 @@
         compiler_params=pltpu.CompilerParams(
             collective_id=0, has_side_effects=True, vmem_limit_bytes=24 * 1024 * 1024
         ),
-    )(right_side, reaction, velocity)
+    )(*[pltpu.with_memory_space_constraint(a, pltpu.HBM) for a in (right_side, reaction, velocity)])
     return sol, res, norm.reshape(())
 
 

time: 89.2 us -> 81.9 us (0.918)
  local copies, waits for them, and re-layouts: 8.6 us -> 2.64 us
  Pallas kernels: 78 us -> 76.8 us
    unnamed x8 -> x2, local copies, waits for them, and re-layouts: 8.6 us -> 2.64 us
    pallas_call x1, Pallas kernels: 78 us -> 76.8 us  [local(): pl.pallas_call(kernel, name='chebyshev', out_shape=(pltpu.VMEM(shape, F32...]
where the time goes in v2:
time: 81.9 us; the launch traced here: 81.7 us
  Pallas kernels  76.8 us (94%)
  local copies, waits for them, and re-layouts  2.64 us (3%)
  between operations  2.33 us (3%)
    pallas_call x1, Pallas kernels, local(): pl.pallas_call(kernel, name='chebyshev', out_shape=(pltpu.VMEM(shape, F32...  76.8 us
    unnamed x2, local copies, waits for them, and re-layouts  2.64 us

profile of v2, /device:TPU:1, one launch (start us, length us, event | category | flops | bytes accessed | tf_op | source)
XLA Modules:
  0.0 81.7 jit_solution(5687909334491913838)
XLA Ops:
  0.6 76.8 %chebyshev.1 = (f32[16,64,512]{2,1,0:T(8,128)S(1)}, f32[16,64,512]{2,1,0:T(8,128)S(1)}, f32[1,1]{1,0:T(1,128)}) custom-call(f32[16,64,512]{2,1,0:T(8,128)} %rhs.1, f32[16,64,512]{2,1,0:T(8,128)} %rea.1, f32[3,16,64,512]{3,2,1,0:T(8,128)} %vel.1), custom_call_target="tpu_custom_call" | custom-call | tf_op jit(solution)/shard_map/chebyshev/pallas_call | solution.py:330
  77.4 1.3 %copy.9 = f32[16,64,512]{2,1,0:T(8,128)} copy(f32[16,64,512]{2,1,0:T(8,128)S(1)} %get-tuple-element.9) | data formatting | bytes 4194304
  78.7 1.3 %copy.10 = f32[16,64,512]{2,1,0:T(8,128)} copy(f32[16,64,512]{2,1,0:T(8,128)S(1)} %get-tuple-element.10) | data formatting | bytes 4194304

commit v3 on v2

v3 whole, which is shorter than its diff:
```python
import functools

import jax
import jax.numpy as jnp
from jax import lax
from jax.experimental import pallas as pl
from jax.experimental.pallas import tpu as pltpu
from jax.sharding import PartitionSpec as P

ITERS = 5
centre = 7.25
half_width = 6.75
MESH = pl.DeviceIdType.MESH
F32 = jnp.float32


def chebyshev_weights(count):
    ratio_value = centre / half_width
    weights = [1.0 / ratio_value]
    for iteration in range(count):
        weights.append(1.0 / (2.0 * ratio_value - weights[-1]))
    return weights


NXL, NYL, NT = 16, 64, 4
NJ = NYL // 8
TOP = 8
CELLS = 256 * 256 * 1024


def kernel(
    rhs, rea, vel, sol, res, norm,
    D0, D1, R, S, V, C, ZS, ZH, G1, G2,
    lf, lr, lc, lv, xs, xr, ys, yr, zs, zr, g1s, g1r, g2s, g2r,
):
    gx, gy, gz = lax.axis_index("gx"), lax.axis_index("gy"), lax.axis_index("gz")
    px, py = gx // 4, gx % 4
    yz = gy * 2 + gz
    weights = chebyshev_weights(ITERS)
    D = (D0, D1)

    def rhs_load(x0, n, t, sem):
        return pltpu.make_async_copy(
            rhs.at[pl.ds(x0, n), :, pl.ds(128 * t, 128)],
            D0.at[pl.ds(x0 + 1, n), t, pl.ds(TOP, NYL), :],
            sem,
        )

    face_loads = [rhs_load(x0, 1, t, lf.at[i, t]) for t in range(NT) for i, x0 in enumerate((0, NXL - 1))]
    rest = [rhs_load(1, NXL - 2, t, lr.at[t]) for t in range(NT)]
    coef = [
        pltpu.make_async_copy(rea.at[:, :, pl.ds(128 * t, 128)], C.at[:, t], lc.at[t]) for t in range(NT)
    ] + [
        pltpu.make_async_copy(vel.at[c, :, :, pl.ds(128 * t, 128)], V.at[c, :, t], lv.at[c, t])
        for t in range(NT)
        for c in range(3)
    ]
    for copy in face_loads + rest + coef:
        copy.start()

    barrier = pltpu.get_barrier_semaphore()
    near = [(gx + 1) % 16, (gx + 15) % 16]
    ring_y = [px * 4 + (py + o) % 4 for o in (1, 2, 3)]
    ring_x = [(gx + 4 * o) % 16 for o in (1, 2, 3)]
    block = [(yz + o) % 8 for o in range(1, 8)]
    peers = [(g, gy, gz) for g in near + ring_y + ring_x] + [(gx, b // 2, b % 2) for b in block]
    for peer in peers:
        pl.semaphore_signal(barrier, inc=1, device_id=peer, device_id_type=MESH)

    zrow = jnp.zeros((1, 128), F32)

    def zero_rows(row):
        def body(x, carry):
            for b in range(2):
                for t in range(NT):
                    D[b][x, t, pl.ds(row, 1), :] = zrow
            return carry

        lax.fori_loop(1, NXL + 1, body, 0)

    @pl.when(gy == 0)
    def _():
        zero_rows(TOP - 1)

    @pl.when(gy == 3)
    def _():
        zero_rows(TOP + NYL)

    for copy in face_loads:
        copy.wait()
    pl.semaphore_wait(barrier, len(peers))

    x_side = (
        (1, NXL + 1, (gx + 15) % 16),
        (NXL, 0, (gx + 1) % 16),
    )

    def x_copy(buf, side, t):
        src, dst, to = x_side[side]
        return pltpu.make_async_remote_copy(
            src_ref=D[buf].at[src, t, pl.ds(TOP, NYL), :],
            dst_ref=D[buf].at[dst, t, pl.ds(TOP, NYL), :],
            send_sem=xs.at[buf, side, t],
            recv_sem=xr.at[buf, side, t],
            device_id=(to, gy, gz),
            device_id_type=MESH,
        )

    y_side = (
        (TOP, TOP + NYL, gy - 1, gy > 0, gy < 3),
        (TOP + NYL - 1, TOP - 1, gy + 1, gy < 3, gy > 0),
    )

    def y_copies(buf, side, chunk):
        src, dst, to, _, _ = y_side[side]
        if chunk == 0:
            parts = [(pl.ds(2, NXL - 2), slice(None), 0)]
        else:
            parts = [(pl.ds(x, 1), pl.ds(chunk - 1, 1), i) for i, x in enumerate((1, NXL))]
        return [
            pltpu.make_async_remote_copy(
                src_ref=D[buf].at[xs_, ts_, pl.ds(src, 1), :],
                dst_ref=D[buf].at[xs_, ts_, pl.ds(dst, 1), :],
                send_sem=ys.at[buf, side, chunk, i],
                recv_sem=yr.at[buf, side, chunk, i],
                device_id=(gx, to, gz),
                device_id_type=MESH,
            )
            for xs_, ts_, i in parts
        ]

    def y_each(buf, chunk, what):
        def act(side):
            for copy in y_copies(buf, side, chunk):
                getattr(copy, what)()

        for side in range(2):
            sends, gets = y_side[side][3:]
            pl.when(gets if what == "wait_recv" else sends)(functools.partial(act, side))

    def z_copy(buf, part):
        return pltpu.make_async_remote_copy(
            src_ref=ZS.at[buf, part],
            dst_ref=ZH.at[buf, part],
            send_sem=zs.at[buf, part],
            recv_sem=zr.at[buf, part],
            device_id=(gx, gy, 1 - gz),
            device_id_type=MESH,
        )

    lane = lax.broadcasted_iota(jnp.int32, (8, 128), 1)
    first_lane, last_lane = lane == 0, lane == 127
    z_tile = (NT - 1) * (1 - gz)
    low = gz.astype(F32)
    high = 1.0 - low

    def z_pack(buf, part):
        def add(x, acc):
            for j in range(NJ):
                v = (x - 1) * NJ + j
                cell = D[buf][x, z_tile, pl.ds(TOP + 8 * j, 8), :]
                cell = pltpu.roll(cell, (v + 1 - gz) & 127, 1)
                acc = jnp.where(lane == v, cell, acc)
            return acc

        def body(i, accs):
            return tuple(add(2 + 7 * a + i, acc) for a, acc in enumerate(accs))

        zero = jnp.zeros((8, 128), F32)
        if part == 0:
            first, second = lax.fori_loop(0, (NXL - 2) // 2, body, (zero, zero))
            ZS[buf, 0] = first + second
        else:
            ZS[buf, 1] = add(1, zero) + add(NXL, zero)

    def row_group(step, x, j, tiles, halo, sums=None):
        now, new = D[step % 2], D[(step + 1) % 2]
        row = TOP + 8 * j
        lines = pl.ds(8 * j, 8)
        cells, ups, downs, stores = {}, {}, {}, []

        def cell(t):
            if t not in cells:
                cells[t] = now[x, t, pl.ds(row, 8), :]
            return cells[t]

        def up(t):
            if t not in ups:
                ups[t] = pltpu.roll(cell(t), 127, 1)
            return ups[t]

        def down(t):
            if t not in downs:
                downs[t] = pltpu.roll(cell(t), 1, 1)
            return downs[t]

        if 0 in tiles or NT - 1 in tiles:
            v = (x - 1) * NJ + j
            beyond = pltpu.roll(halo, (127 * (1 - gz) - v) & 127, 1)
        for t in tiles:
            m = cell(t)
            zm = jnp.where(first_lane, down(t - 1) if t else beyond * low, down(t))
            zp = jnp.where(last_lane, up(t + 1) if t < NT - 1 else beyond * high, up(t))
            xm = now[x - 1, t, pl.ds(row, 8), :]
            xp = now[x + 1, t, pl.ds(row, 8), :]
            ym = now[x, t, pl.ds(row - 1, 8), :]
            yp = now[x, t, pl.ds(row + 1, 8), :]
            at = (x - 1, t, lines, slice(None))
            vx, vy, vz = (V[(c,) + at] for c in range(3))
            flow = vx * (xp - xm) + vy * (yp - ym) + vz * (zp - zm)
            beside = ((xp + xm) + (yp + ym)) + (zp + zm)
            applied = (6.0 + C[at]) * m - (beside - flow)
            out = (x - 1, lines, pl.ds(128 * t, 128))
            if step == 0:
                r = m - applied * (1.0 / centre)
                alpha = weights[1] * weights[0] / centre
            else:
                r = R[at] - applied
                alpha = weights[step + 1] * weights[step] if step + 1 < ITERS else 0.0
            if step + 1 < ITERS:
                d = alpha * m + (2.0 * weights[step + 1] / half_width) * r
                s = (m * (1.0 / centre) if step == 0 else S[at]) + d
                stores.append((R, at, r))
                stores.append((new, (x, t, pl.ds(row, 8), slice(None)), d))
                stores.append((S, at, s) if step + 2 < ITERS else (sol, out, s))
            else:
                stores.append((res, out, r))
                sums[t] = sums[t] + r * r
        return stores

    def groups(step, items, halo, sums=None):
        held = []
        for x, j, tiles in items:
            stores = row_group(step, x, j, tiles, halo, sums)
            for ref, at, value in held:
                ref[at] = value
            held = stores
        for ref, at, value in held:
            ref[at] = value

    def layers(step, js, halo, many):
        def body(i, carry):
            groups(step, [(2 + i * many + k, j, range(NT)) for k in range(many) for j in js], halo)
            return carry

        lax.fori_loop(0, (NXL - 2) // many, body, 0)

    def faces(step, t, sums=None):
        groups(step, [(x, j, (t,)) for j in range(NJ) for x in (1, NXL)], ZH[step % 2, 1], sums)

    for t in range(NT):
        for side in range(2):
            x_copy(0, side, t).start()
    for copy in rest:
        copy.wait()
    for chunk in range(NT + 1):
        y_each(0, chunk, "start")
    for part in range(2):
        z_pack(0, part)
        z_copy(0, part).start()
    for copy in coef:
        copy.wait()

    for step in range(ITERS - 1):
        cur, new = step % 2, (step + 1) % 2
        y_each(cur, 0, "wait_recv")
        z_copy(cur, 0).wait_recv()
        halo = ZH[cur, 0]
        layers(step, (0, NJ - 1), halo, 7)
        y_each(new, 0, "start")
        layers(step, range(1, NJ - 1), halo, 2)
        z_pack(new, 0)
        z_copy(new, 0).start()
        z_copy(cur, 1).wait_recv()
        for t in range(NT):
            for side in range(2):
                x_copy(cur, side, t).wait_recv()
            y_each(cur, t + 1, "wait_recv")
            faces(step, t)
            for side in range(2):
                x_copy(new, side, t).start()
            y_each(new, t + 1, "start")
        z_pack(new, 1)
        z_copy(new, 1).start()
        for t in range(NT):
            for side in range(2):
                x_copy(cur, side, t).wait_send()
        for chunk in range(NT + 1):
            y_each(cur, chunk, "wait_send")
        for part in range(2):
            z_copy(cur, part).wait_send()

    step = ITERS - 1
    cur = step % 2
    y_each(cur, 0, "wait_recv")
    z_copy(cur, 0).wait_recv()
    halo = ZH[cur, 0]

    def last_layers(i, sums):
        sums = list(sums)
        groups(step, [(2 + 2 * i + k, j, range(NT)) for k in range(2) for j in range(NJ)], halo, sums)
        return tuple(sums)

    zero = jnp.zeros((8, 128), F32)
    sums = list(lax.fori_loop(0, (NXL - 2) // 2, last_layers, (zero,) * NT))
    z_copy(cur, 1).wait_recv()
    for t in range(NT):
        for side in range(2):
            x_copy(cur, side, t).wait_recv()
        y_each(cur, t + 1, "wait_recv")
        faces(step, t, sums)
    total = (sums[0] + sums[1]) + (sums[2] + sums[3])

    def stage(total, G, send, recv, own, count, place):
        G[own] = total
        copies = [
            pltpu.make_async_remote_copy(
                src_ref=G.at[own],
                dst_ref=G.at[own],
                send_sem=send.at[o - 1],
                recv_sem=recv.at[o - 1],
                device_id=place((own + o) % count),
                device_id_type=MESH,
            )
            for o in range(1, count)
        ]
        for copy in copies:
            copy.start()
        for copy in copies:
            copy.wait_recv()
        total = G[0]
        for i in range(1, count):
            total = total + G[i]
        return total, copies

    total, c1 = stage(total, G1, g1s, g1r, gx, 16, lambda p: (p, gy, gz))
    total, c2 = stage(total, G2, g2s, g2r, yz, 8, lambda p: (gx, p // 2, p % 2))
    whole = jnp.sum(jnp.sum(total, axis=0, keepdims=True), axis=1, keepdims=True)
    norm[...] = jnp.sqrt(whole * (1.0 / CELLS) + 1e-06)
    for t in range(NT):
        for side in range(2):
            x_copy(cur, side, t).wait_send()
    for chunk in range(NT + 1):
        y_each(cur, chunk, "wait_send")
    for part in range(2):
        z_copy(cur, part).wait_send()
    for copy in c1 + c2:
        copy.wait_send()


def local(right_side, reaction, velocity):
    sem = pltpu.SemaphoreType.DMA
    shape = right_side.shape
    sol, res, norm = pl.pallas_call(
        kernel,
        name="chebyshev",
        out_shape=(pltpu.VMEM(shape, F32), pltpu.VMEM(shape, F32), jax.ShapeDtypeStruct((1, 1), F32)),
        in_specs=[pl.BlockSpec(memory_space=pltpu.HBM)] * 3,
        out_specs=(pl.BlockSpec(memory_space=pltpu.VMEM),) * 3,
        scratch_shapes=[
            pltpu.VMEM((NXL + 2, NT, NYL + 16, 128), F32),
            pltpu.VMEM((NXL + 2, NT, NYL + 16, 128), F32),
            pltpu.VMEM((NXL, NT, NYL, 128), F32),
            pltpu.VMEM((NXL, NT, NYL, 128), F32),
            pltpu.VMEM((3, NXL, NT, NYL, 128), F32),
            pltpu.VMEM((NXL, NT, NYL, 128), F32),
            pltpu.VMEM((2, 2, 8, 128), F32),
            pltpu.VMEM((2, 2, 8, 128), F32),
            pltpu.VMEM((16, 8, 128), F32),
            pltpu.VMEM((8, 8, 128), F32),
            sem((2, NT)), sem((NT,)), sem((NT,)), sem((3, NT)),
            sem((2, 2, NT)), sem((2, 2, NT)), sem((2, 2, NT + 1, 2)), sem((2, 2, NT + 1, 2)),
            sem((2, 2)), sem((2, 2)), sem((15,)), sem((15,)), sem((7,)), sem((7,)),
        ],
        compiler_params=pltpu.CompilerParams(
            collective_id=0, has_side_effects=True, vmem_limit_bytes=24 * 1024 * 1024
        ),
    )(*[pltpu.with_memory_space_constraint(a, pltpu.HBM) for a in (right_side, reaction, velocity)])
    return sol, res, norm.reshape(())


def solution(mesh):
    spec = P("gx", "gy", "gz")
    return jax.shard_map(
        local,
        mesh=mesh,
        in_specs=(spec, spec, P(None, "gx", "gy", "gz")),
        out_specs=(spec, spec, P()),
        check_vma=False,
    )
```

time: 81.9 us -> 51.3 us (0.63)
  Pallas kernels: 76.8 us -> 46.2 us
    pallas_call x1, Pallas kernels: 76.8 us -> 46.2 us  [local(): pl.pallas_call(kernel, name='chebyshev', out_shape=(pltpu.VMEM(shape, F32...]
where the time goes in v3:
time: 51.3 us; the launch traced here: 51.1 us
  Pallas kernels  46.2 us (90%)
  local copies, waits for them, and re-layouts  2.64 us (5%)
  between operations  2.33 us (5%)
    pallas_call x1, Pallas kernels, local(): pl.pallas_call(kernel, name='chebyshev', out_shape=(pltpu.VMEM(shape, F32...  46.2 us
    unnamed x2, local copies, waits for them, and re-layouts  2.64 us

profile of v3, /device:TPU:1, one launch (start us, length us, event | category | flops | bytes accessed | tf_op | source)
XLA Modules:
  0.0 51.1 jit_solution(3856746385823265483)
XLA Ops:
  0.6 46.2 %chebyshev.1 = (f32[16,64,512]{2,1,0:T(8,128)S(1)}, f32[16,64,512]{2,1,0:T(8,128)S(1)}, f32[1,1]{1,0:T(1,128)}) custom-call(f32[16,64,512]{2,1,0:T(8,128)} %rhs.1, f32[16,64,512]{2,1,0:T(8,128)} %rea.1, f32[3,16,64,512]{3,2,1,0:T(8,128)} %vel.1), custom_call_target="tpu_custom_call" | custom-call | tf_op jit(solution)/shard_map/chebyshev/pallas_call | solution.py:354
  46.8 1.3 %copy.9 = f32[16,64,512]{2,1,0:T(8,128)} copy(f32[16,64,512]{2,1,0:T(8,128)S(1)} %get-tuple-element.9) | data formatting | bytes 4194304
  48.1 1.3 %copy.10 = f32[16,64,512]{2,1,0:T(8,128)} copy(f32[16,64,512]{2,1,0:T(8,128)S(1)} %get-tuple-element.10) | data formatting | bytes 4194304

commit v4 on v3

v4 whole, which is shorter than its diff:
```python
import functools

import jax
import jax.numpy as jnp
from jax import lax
from jax.experimental import pallas as pl
from jax.experimental.pallas import tpu as pltpu
from jax.sharding import PartitionSpec as P

ITERS = 5
centre = 7.25
half_width = 6.75
MESH = pl.DeviceIdType.MESH
F32 = jnp.float32


def chebyshev_weights(count):
    ratio_value = centre / half_width
    weights = [1.0 / ratio_value]
    for iteration in range(count):
        weights.append(1.0 / (2.0 * ratio_value - weights[-1]))
    return weights


NXL, NYL, NT = 16, 64, 4
NJ = NYL // 8
TOP = 8
NH = 2
CELLS = 256 * 256 * 1024
SLABS = ((1, 6), (7, 4), (11, 4), (0, 1), (15, 1))


def kernel(
    rhs, rea, vel, sol, res, norm,
    D0, D1, R, S, V, C, ZS, ZH, G1, G2,
    lf, lr, lc, lv, xs, xr, ys, yr, zs, zr, g1s, g1r, g2s, g2r,
):
    gx, gy, gz = lax.axis_index("gx"), lax.axis_index("gy"), lax.axis_index("gz")
    px, py = gx // 4, gx % 4
    yz = gy * 2 + gz
    weights = chebyshev_weights(ITERS)
    D = (D0, D1)

    barrier = pltpu.get_barrier_semaphore()
    near = [(gx + 1) % 16, (gx + 15) % 16]
    ring_y = [px * 4 + (py + o) % 4 for o in (1, 2, 3)]
    ring_x = [(gx + 4 * o) % 16 for o in (1, 2, 3)]
    block = [(yz + o) % 8 for o in range(1, 8)]
    peers = [(g, gy, gz) for g in near + ring_y + ring_x] + [(gx, b // 2, b % 2) for b in block]
    for peer in peers:
        pl.semaphore_signal(barrier, inc=1, device_id=peer, device_id_type=MESH)

    def rhs_load(x0, n, t, sem):
        return pltpu.make_async_copy(
            rhs.at[pl.ds(x0, n), :, pl.ds(128 * t, 128)],
            D0.at[pl.ds(x0 + 1, n), t, pl.ds(TOP, NYL), :],
            sem,
        )

    face_loads = [rhs_load(x0, 1, t, lf.at[i, t]) for t in range(NT) for i, x0 in enumerate((0, NXL - 1))]
    rest = [rhs_load(1, NXL - 2, t, lr.at[t]) for t in range(NT)]

    def coef_load(x0, n, i):
        out = []
        for t in range(NT):
            lanes = pl.ds(128 * t, 128)
            out.append(pltpu.make_async_copy(rea.at[pl.ds(x0, n), :, lanes], C.at[pl.ds(x0, n), t], lc.at[i, t]))
            out += [
                pltpu.make_async_copy(
                    vel.at[c, pl.ds(x0, n), :, lanes], V.at[c, pl.ds(x0, n), t], lv.at[i, c, t]
                )
                for c in range(3)
            ]
        return out

    slabs = [coef_load(x0, n, i) for i, (x0, n) in enumerate(SLABS)]
    for copy in face_loads + rest + sum(slabs, []):
        copy.start()

    zrow = jnp.zeros((1, 128), F32)

    def zero_rows(row):
        def body(x, carry):
            for b in range(2):
                for t in range(NT):
                    D[b][x, t, pl.ds(row, 1), :] = zrow
            return carry

        lax.fori_loop(1, NXL + 1, body, 0)

    @pl.when(gy == 0)
    def _():
        zero_rows(TOP - 1)

    @pl.when(gy == 3)
    def _():
        zero_rows(TOP + NYL)

    for copy in face_loads:
        copy.wait()
    pl.semaphore_wait(barrier, len(peers))

    x_side = (
        (1, NXL + 1, (gx + 15) % 16),
        (NXL, 0, (gx + 1) % 16),
    )

    def tile(t):
        return t + gz * (NT - 1 - 2 * t)

    def x_copy(buf, side, t, h):
        src, dst, to = x_side[side]
        rows = pl.ds(TOP + h * (NYL // NH), NYL // NH)
        return pltpu.make_async_remote_copy(
            src_ref=D[buf].at[src, tile(t), rows, :],
            dst_ref=D[buf].at[dst, tile(t), rows, :],
            send_sem=xs.at[buf, side, t, h],
            recv_sem=xr.at[buf, side, t, h],
            device_id=(to, gy, gz),
            device_id_type=MESH,
        )

    def x_each(buf, t, h, what):
        for side in range(2):
            getattr(x_copy(buf, side, t, h), what)()

    chunks = [(t, h) for t in range(NT) for h in range(NH)]

    y_side = (
        (TOP, TOP + NYL, gy - 1, gy > 0, gy < 3),
        (TOP + NYL - 1, TOP - 1, gy + 1, gy < 3, gy > 0),
    )

    def y_copies(buf, side, chunk):
        src, dst, to, _, _ = y_side[side]
        if chunk == 0:
            parts = [(pl.ds(2, NXL - 2), slice(None), 0)]
        else:
            parts = [(pl.ds(x, 1), pl.ds(tile(chunk - 1), 1), i) for i, x in enumerate((1, NXL))]
        return [
            pltpu.make_async_remote_copy(
                src_ref=D[buf].at[xs_, ts_, pl.ds(src, 1), :],
                dst_ref=D[buf].at[xs_, ts_, pl.ds(dst, 1), :],
                send_sem=ys.at[buf, side, chunk, i],
                recv_sem=yr.at[buf, side, chunk, i],
                device_id=(gx, to, gz),
                device_id_type=MESH,
            )
            for xs_, ts_, i in parts
        ]

    def y_each(buf, chunk, what, which=(0, 1)):
        def act(side):
            for copy in y_copies(buf, side, chunk):
                getattr(copy, what)()

        for side in which:
            sends, gets = y_side[side][3:]
            pl.when(gets if what == "wait_recv" else sends)(functools.partial(act, side))

    def z_copy(buf, part):
        return pltpu.make_async_remote_copy(
            src_ref=ZS.at[buf, part],
            dst_ref=ZH.at[buf, part],
            send_sem=zs.at[buf, part],
            recv_sem=zr.at[buf, part],
            device_id=(gx, gy, 1 - gz),
            device_id_type=MESH,
        )

    lane = lax.broadcasted_iota(jnp.int32, (8, 128), 1)
    first_lane, last_lane = lane == 0, lane == 127
    z_tile = (NT - 1) * (1 - gz)
    low = gz.astype(F32)
    high = 1.0 - low

    def z_pack(buf, part):
        def add(x, acc):
            for j in range(NJ):
                v = (x - 1) * NJ + j
                cell = D[buf][x, z_tile, pl.ds(TOP + 8 * j, 8), :]
                cell = pltpu.roll(cell, (v + 1 - gz) & 127, 1)
                acc = jnp.where(lane == v, cell, acc)
            return acc

        def body(i, accs):
            return tuple(add(2 + 7 * a + i, acc) for a, acc in enumerate(accs))

        zero = jnp.zeros((8, 128), F32)
        if part == 0:
            first, second = lax.fori_loop(0, (NXL - 2) // 2, body, (zero, zero))
            ZS[buf, 0] = first + second
        else:
            ZS[buf, 1] = add(1, zero) + add(NXL, zero)

    def row_group(step, x, j, tiles, halo, sums=None):
        now = D[step % 2]
        row = TOP + 8 * j
        lines = pl.ds(8 * j, 8)
        cells, ups, downs, stores = {}, {}, {}, []

        def cell(t):
            if t not in cells:
                cells[t] = now[x, t, pl.ds(row, 8), :]
            return cells[t]

        def up(t):
            if t not in ups:
                ups[t] = pltpu.roll(cell(t), 127, 1)
            return ups[t]

        def down(t):
            if t not in downs:
                downs[t] = pltpu.roll(cell(t), 1, 1)
            return downs[t]

        if 0 in tiles or NT - 1 in tiles:
            v = (x - 1) * NJ + j
            beyond = pltpu.roll(halo, (127 * (1 - gz) - v) & 127, 1)
        for t in tiles:
            m = cell(t)
            zm = jnp.where(first_lane, down(t - 1) if t else beyond * low, down(t))
            zp = jnp.where(last_lane, up(t + 1) if t < NT - 1 else beyond * high, up(t))
            stores += cell_step(step, x, t, row, lines, m, zm, zp, sums, t)
        return stores

    def face_group(step, x, j, t, halo, sums=None):
        now = D[step % 2]
        row = TOP + 8 * j
        lines, rows = pl.ds(8 * j, 8), pl.ds(row, 8)
        at_t = tile(t)
        m = now[x, at_t, rows, :]
        down, up = pltpu.roll(m, 1, 1), pltpu.roll(m, 127, 1)
        before = pltpu.roll(now[x, jnp.maximum(at_t - 1, 0), rows, :], 1, 1)
        after = pltpu.roll(now[x, jnp.minimum(at_t + 1, NT - 1), rows, :], 127, 1)
        if t == 0:
            before, after = before * low, after * high
        if t == NT - 1:
            v = (x - 1) * NJ + j
            beyond = pltpu.roll(halo, (127 * (1 - gz) - v) & 127, 1)
            before = before * high + beyond * low
            after = after * low + beyond * high
        zm = jnp.where(first_lane, before, down)
        zp = jnp.where(last_lane, after, up)
        return cell_step(step, x, at_t, row, lines, m, zm, zp, sums, t)

    def cell_step(step, x, t, row, lines, m, zm, zp, sums, slot):
        now, new = D[step % 2], D[(step + 1) % 2]
        xm = now[x - 1, t, pl.ds(row, 8), :]
        xp = now[x + 1, t, pl.ds(row, 8), :]
        ym = now[x, t, pl.ds(row - 1, 8), :]
        yp = now[x, t, pl.ds(row + 1, 8), :]
        at = (x - 1, t, lines, slice(None))
        vx, vy, vz = (V[(c,) + at] for c in range(3))
        flow = vx * (xp - xm) + vy * (yp - ym) + vz * (zp - zm)
        beside = ((xp + xm) + (yp + ym)) + (zp + zm)
        applied = (6.0 + C[at]) * m - (beside - flow)
        lanes = pl.ds(128 * t if isinstance(t, int) else pl.multiple_of(128 * t, 128), 128)
        out = (x - 1, lines, lanes)
        if step == 0:
            r = m - applied * (1.0 / centre)
            alpha = weights[1] * weights[0] / centre
        else:
            r = R[at] - applied
            alpha = weights[step + 1] * weights[step] if step + 1 < ITERS else 0.0
        if step + 1 == ITERS:
            sums[slot] = sums[slot] + r * r
            return [(res, out, r)]
        d = alpha * m + (2.0 * weights[step + 1] / half_width) * r
        s = (m * (1.0 / centre) if step == 0 else S[at]) + d
        return [
            (R, at, r),
            (new, (x, t, pl.ds(row, 8), slice(None)), d),
            (S, at, s) if step + 2 < ITERS else (sol, out, s),
        ]

    def late(parts):
        held = []
        for part in parts:
            stores = part()
            for ref, at, value in held:
                ref[at] = value
            held = stores
        for ref, at, value in held:
            ref[at] = value

    def groups(step, items, halo, sums=None):
        late([functools.partial(row_group, step, x, j, range(NT), halo, sums) for x, j in items])

    def layers(step, first, count, js, halo, many):
        def body(i, carry):
            groups(step, [(first + i * many + k, j) for k in range(many) for j in js], halo)
            return carry

        lax.fori_loop(0, count // many, body, 0)

    def faces(step, t, h, sums=None):
        js = range(h * (NJ // NH), (h + 1) * (NJ // NH))
        halo = ZH[step % 2, 1]
        late([functools.partial(face_group, step, x, j, t, halo, sums) for j in js for x in (1, NXL)])

    for t, h in chunks:
        x_each(0, t, h, "start")
    for copy in rest:
        copy.wait()
    for chunk in range(NT + 1):
        y_each(0, chunk, "start")
    for part in range(2):
        z_pack(0, part)
        z_copy(0, part).start()

    for step in range(ITERS):
        cur, new, more = step % 2, (step + 1) % 2, step + 1 < ITERS
        y_each(cur, 0, "wait_recv")
        z_copy(cur, 0).wait_recv()
        halo = ZH[cur, 0]
        sums = None
        if step == 0:
            for (x0, n), slab in list(zip(SLABS, slabs))[:3]:
                for copy in slab:
                    copy.wait()
                layers(step, x0 + 1, n, range(NJ), halo, 2)
            y_each(new, 0, "start")
        elif more:
            layers(step, 2, NXL - 2, (0, NJ - 1), halo, 7)
            y_each(new, 0, "start")
            layers(step, 2, NXL - 2, range(1, NJ - 1), halo, 2)
        else:

            def last_layers(i, sums):
                sums = list(sums)
                groups(step, [(2 + 2 * i + k, j) for k in range(2) for j in range(NJ)], halo, sums)
                return tuple(sums)

            zero = jnp.zeros((8, 128), F32)
            sums = list(lax.fori_loop(0, (NXL - 2) // 2, last_layers, (zero,) * NT))
        if more:
            z_pack(new, 0)
            z_copy(new, 0).start()
        if step == 0:
            for copy in slabs[3] + slabs[4]:
                copy.wait()
        for t, h in chunks:
            x_each(cur, t, h, "wait_recv")
            if h == 0:
                y_each(cur, t + 1, "wait_recv", (1,))
            if h == NH - 1:
                y_each(cur, t + 1, "wait_recv", (0,))
            if (t, h) == (NT - 1, 0):
                z_copy(cur, 1).wait_recv()
            faces(step, t, h, sums)
            if more:
                x_each(new, t, h, "start")
                if h == 0:
                    y_each(new, t + 1, "start", (0,))
                if h == NH - 1:
                    y_each(new, t + 1, "start", (1,))
        if more:
            z_pack(new, 1)
            z_copy(new, 1).start()
            for t, h in chunks:
                x_each(cur, t, h, "wait_send")
            for chunk in range(NT + 1):
                y_each(cur, chunk, "wait_send")
            for part in range(2):
                z_copy(cur, part).wait_send()
    total = jnp.sum((sums[0] + sums[1]) + (sums[2] + sums[3]), axis=0, keepdims=True)

    def stage(total, G, send, recv, own, count, place):
        G[own, pl.ds(0, 1), :] = total
        copies = [
            pltpu.make_async_remote_copy(
                src_ref=G.at[own, pl.ds(0, 1), :],
                dst_ref=G.at[own, pl.ds(0, 1), :],
                send_sem=send.at[o - 1],
                recv_sem=recv.at[o - 1],
                device_id=place((own + o) % count),
                device_id_type=MESH,
            )
            for o in range(1, count)
        ]
        for copy in copies:
            copy.start()
        for copy in copies:
            copy.wait_recv()
        parts = [G[i, pl.ds(0, 1), :] for i in range(count)]
        while len(parts) > 1:
            parts = [a + b for a, b in zip(parts[::2], parts[1::2])]
        return parts[0], copies

    total, c1 = stage(total, G1, g1s, g1r, gx, 16, lambda p: (p, gy, gz))
    total, c2 = stage(total, G2, g2s, g2r, yz, 8, lambda p: (gx, p // 2, p % 2))
    whole = jnp.sum(total, axis=1, keepdims=True)
    norm[...] = jnp.sqrt(whole * (1.0 / CELLS) + 1e-06)
    cur = (ITERS - 1) % 2
    for t, h in chunks:
        x_each(cur, t, h, "wait_send")
    for chunk in range(NT + 1):
        y_each(cur, chunk, "wait_send")
    for part in range(2):
        z_copy(cur, part).wait_send()
    for copy in c1 + c2:
        copy.wait_send()


def local(right_side, reaction, velocity):
    sem = pltpu.SemaphoreType.DMA
    shape = right_side.shape
    sol, res, norm = pl.pallas_call(
        kernel,
        name="chebyshev",
        out_shape=(pltpu.VMEM(shape, F32), pltpu.VMEM(shape, F32), jax.ShapeDtypeStruct((1, 1), F32)),
        in_specs=[pl.BlockSpec(memory_space=pltpu.HBM)] * 3,
        out_specs=(pl.BlockSpec(memory_space=pltpu.VMEM),) * 3,
        scratch_shapes=[
            pltpu.VMEM((NXL + 2, NT, NYL + 16, 128), F32),
            pltpu.VMEM((NXL + 2, NT, NYL + 16, 128), F32),
            pltpu.VMEM((NXL, NT, NYL, 128), F32),
            pltpu.VMEM((NXL, NT, NYL, 128), F32),
            pltpu.VMEM((3, NXL, NT, NYL, 128), F32),
            pltpu.VMEM((NXL, NT, NYL, 128), F32),
            pltpu.VMEM((2, 2, 8, 128), F32),
            pltpu.VMEM((2, 2, 8, 128), F32),
            pltpu.VMEM((16, 8, 128), F32),
            pltpu.VMEM((8, 8, 128), F32),
            sem((2, NT)), sem((NT,)), sem((5, NT)), sem((5, 3, NT)),
            sem((2, 2, NT, NH)), sem((2, 2, NT, NH)), sem((2, 2, NT + 1, 2)), sem((2, 2, NT + 1, 2)),
            sem((2, 2)), sem((2, 2)), sem((15,)), sem((15,)), sem((7,)), sem((7,)),
        ],
        compiler_params=pltpu.CompilerParams(
            collective_id=0, has_side_effects=True, vmem_limit_bytes=24 * 1024 * 1024
        ),
    )(*[pltpu.with_memory_space_constraint(a, pltpu.HBM) for a in (right_side, reaction, velocity)])
    return sol, res, norm.reshape(())


def solution(mesh):
    spec = P("gx", "gy", "gz")
    return jax.shard_map(
        local,
        mesh=mesh,
        in_specs=(spec, spec, P(None, "gx", "gy", "gz")),
        out_specs=(spec, spec, P()),
        check_vma=False,
    )
```

time: 51.3 us -> 51.6 us (level)
  no operation moved by 1% of the time
where the time goes in v4:
time: 51.6 us; the launch traced here: 51.5 us
  Pallas kernels  46.5 us (90%)
  local copies, waits for them, and re-layouts  2.64 us (5%)
  between operations  2.33 us (5%)
    pallas_call x1, Pallas kernels, local(): pl.pallas_call(kernel, name='chebyshev', out_shape=(pltpu.VMEM(shape, F32...  46.5 us
    unnamed x2, local copies, waits for them, and re-layouts  2.64 us

profile of v4, /device:TPU:1, one launch (start us, length us, event | category | flops | bytes accessed | tf_op | source)
XLA Modules:
  0.0 51.5 jit_solution(536858708272833464)
XLA Ops:
  0.6 46.5 %chebyshev.1 = (f32[16,64,512]{2,1,0:T(8,128)S(1)}, f32[16,64,512]{2,1,0:T(8,128)S(1)}, f32[1,1]{1,0:T(1,128)}) custom-call(f32[16,64,512]{2,1,0:T(8,128)} %rhs.1, f32[16,64,512]{2,1,0:T(8,128)} %rea.1, f32[3,16,64,512]{3,2,1,0:T(8,128)} %vel.1), custom_call_target="tpu_custom_call" | custom-call | tf_op jit(solution)/shard_map/chebyshev/pallas_call | solution.py:409
  47.1 1.3 %copy.9 = f32[16,64,512]{2,1,0:T(8,128)} copy(f32[16,64,512]{2,1,0:T(8,128)S(1)} %get-tuple-element.9) | data formatting | bytes 4194304
  48.5 1.3 %copy.10 = f32[16,64,512]{2,1,0:T(8,128)} copy(f32[16,64,512]{2,1,0:T(8,128)S(1)} %get-tuple-element.10) | data formatting | bytes 4194304

commit v5 on v4

--- a/solution.py
+++ b/solution.py
@@ -27,7 +27,7 @@
 TOP = 8
 NH = 2
 CELLS = 256 * 256 * 1024
-SLABS = ((1, 6), (7, 4), (11, 4), (0, 1), (15, 1))
+SLABS = ((0, 1), (15, 1), (1, 4), (5, 4), (9, 6))
 
 
 def kernel(
@@ -174,24 +174,29 @@
     low = gz.astype(F32)
     high = 1.0 - low
 
+    middle = range(1, NJ - 1)
+
     def z_pack(buf, part):
-        def add(x, acc):
-            for j in range(NJ):
+        def add(x, js, acc):
+            for j in js:
                 v = (x - 1) * NJ + j
                 cell = D[buf][x, z_tile, pl.ds(TOP + 8 * j, 8), :]
                 cell = pltpu.roll(cell, (v + 1 - gz) & 127, 1)
                 acc = jnp.where(lane == v, cell, acc)
             return acc
 
-        def body(i, accs):
-            return tuple(add(2 + 7 * a + i, acc) for a, acc in enumerate(accs))
-
-        zero = jnp.zeros((8, 128), F32)
+        acc = jnp.zeros((8, 128), F32)
         if part == 0:
-            first, second = lax.fori_loop(0, (NXL - 2) // 2, body, (zero, zero))
-            ZS[buf, 0] = first + second
+            acc = lax.fori_loop(0, 4, lambda i, acc: add(3 + 2 * i, range(NJ), add(2 + 2 * i, range(NJ), acc)), acc)
+            for x in range(10, NXL):
+                acc = add(x, (0, NJ - 1), acc)
+        elif part == 1:
+            acc = add(NXL, range(NJ), add(1, range(NJ), acc))
         else:
-            ZS[buf, 1] = add(1, zero) + add(NXL, zero)
+            acc = lax.fori_loop(
+                0, 2, lambda i, acc: add(12 + 3 * i, middle, add(11 + 3 * i, middle, add(10 + 3 * i, middle, acc))), acc
+            )
+        ZS[buf, part] = acc
 
     def row_group(step, x, j, tiles, halo, sums=None):
         now = D[step % 2]
@@ -287,12 +292,13 @@
     def groups(step, items, halo, sums=None):
         late([functools.partial(row_group, step, x, j, range(NT), halo, sums) for x, j in items])
 
-    def layers(step, first, count, js, halo, many):
+    def layers(step, first, count, js, halo, many, sums):
         def body(i, carry):
-            groups(step, [(first + i * many + k, j) for k in range(many) for j in js], halo)
-            return carry
-
-        lax.fori_loop(0, count // many, body, 0)
+            part = list(carry)
+            groups(step, [(first + i * many + k, j) for k in range(many) for j in js], halo, part)
+            return tuple(part)
+
+        sums[:] = lax.fori_loop(0, count // many, body, tuple(sums))
 
     def faces(step, t, h, sums=None):
         js = range(h * (NJ // NH), (h + 1) * (NJ // NH))
@@ -305,7 +311,7 @@
         copy.wait()
     for chunk in range(NT + 1):
         y_each(0, chunk, "start")
-    for part in range(2):
+    for part in range(3):
         z_pack(0, part)
         z_copy(0, part).start()
 
@@ -314,32 +320,26 @@
         y_each(cur, 0, "wait_recv")
         z_copy(cur, 0).wait_recv()
         halo = ZH[cur, 0]
-        sums = None
+        sums = [] if more else [jnp.zeros((8, 128), F32)] * NT
         if step == 0:
-            for (x0, n), slab in list(zip(SLABS, slabs))[:3]:
-                for copy in slab:
-                    copy.wait()
-                layers(step, x0 + 1, n, range(NJ), halo, 2)
+            for copy in slabs[0] + slabs[1] + slabs[2]:
+                copy.wait()
+            layers(step, 2, 4, range(NJ), halo, 2, sums)
+            for copy in slabs[3]:
+                copy.wait()
+            layers(step, 6, 4, range(NJ), halo, 2, sums)
+            for copy in slabs[4]:
+                copy.wait()
+            layers(step, 10, 6, (0, NJ - 1), halo, 6, sums)
             y_each(new, 0, "start")
-        elif more:
-            layers(step, 2, NXL - 2, (0, NJ - 1), halo, 7)
-            y_each(new, 0, "start")
-            layers(step, 2, NXL - 2, range(1, NJ - 1), halo, 2)
         else:
-
-            def last_layers(i, sums):
-                sums = list(sums)
-                groups(step, [(2 + 2 * i + k, j) for k in range(2) for j in range(NJ)], halo, sums)
-                return tuple(sums)
-
-            zero = jnp.zeros((8, 128), F32)
-            sums = list(lax.fori_loop(0, (NXL - 2) // 2, last_layers, (zero,) * NT))
+            layers(step, 2, NXL - 2, (0, NJ - 1), halo, 7, sums)
+            if more:
+                y_each(new, 0, "start")
+            layers(step, 2, 8, middle, halo, 2, sums)
         if more:
             z_pack(new, 0)
             z_copy(new, 0).start()
-        if step == 0:
-            for copy in slabs[3] + slabs[4]:
-                copy.wait()
         for t, h in chunks:
             x_each(cur, t, h, "wait_recv")
             if h == 0:
@@ -355,6 +355,14 @@
                     y_each(new, t + 1, "start", (0,))
                 if h == NH - 1:
                     y_each(new, t + 1, "start", (1,))
+            place = t * NH + h
+            if place == 0:
+                z_copy(cur, 2).wait_recv()
+            if place < 3:
+                groups(step, [(10 + 2 * place + k, j) for k in range(2) for j in middle], ZH[cur, 2], sums)
+            if place == 3 and more:
+                z_pack(new, 2)
+                z_copy(new, 2).start()
         if more:
             z_pack(new, 1)
             z_copy(new, 1).start()
@@ -362,7 +370,7 @@
                 x_each(cur, t, h, "wait_send")
             for chunk in range(NT + 1):
                 y_each(cur, chunk, "wait_send")
-            for part in range(2):
+            for part in range(3):
                 z_copy(cur, part).wait_send()
     total = jnp.sum((sums[0] + sums[1]) + (sums[2] + sums[3]), axis=0, keepdims=True)
 
@@ -397,7 +405,7 @@
         x_each(cur, t, h, "wait_send")
     for chunk in range(NT + 1):
         y_each(cur, chunk, "wait_send")
-    for part in range(2):
+    for part in range(3):
         z_copy(cur, part).wait_send()
     for copy in c1 + c2:
         copy.wait_send()
@@ -419,13 +427,13 @@
             pltpu.VMEM((NXL, NT, NYL, 128), F32),
             pltpu.VMEM((3, NXL, NT, NYL, 128), F32),
             pltpu.VMEM((NXL, NT, NYL, 128), F32),
-            pltpu.VMEM((2, 2, 8, 128), F32),
-            pltpu.VMEM((2, 2, 8, 128), F32),
+            pltpu.VMEM((2, 3, 8, 128), F32),
+            pltpu.VMEM((2, 3, 8, 128), F32),
             pltpu.VMEM((16, 8, 128), F32),
             pltpu.VMEM((8, 8, 128), F32),
             sem((2, NT)), sem((NT,)), sem((5, NT)), sem((5, 3, NT)),
             sem((2, 2, NT, NH)), sem((2, 2, NT, NH)), sem((2, 2, NT + 1, 2)), sem((2, 2, NT + 1, 2)),
-            sem((2, 2)), sem((2, 2)), sem((15,)), sem((15,)), sem((7,)), sem((7,)),
+            sem((2, 3)), sem((2, 3)), sem((15,)), sem((15,)), sem((7,)), sem((7,)),
         ],
         compiler_params=pltpu.CompilerParams(
             collective_id=0, has_side_effects=True, vmem_limit_bytes=24 * 1024 * 1024

time: 51.6 us -> 50.6 us (0.981)
  Pallas kernels: 46.5 us -> 45.5 us
    pallas_call x1, Pallas kernels: 46.5 us -> 45.5 us  [local(): pl.pallas_call(kernel, name='chebyshev', out_shape=(pltpu.VMEM(shape, F32...]
where the time goes in v5:
time: 50.6 us; the launch traced here: 50.5 us
  Pallas kernels  45.5 us (90%)
  local copies, waits for them, and re-layouts  2.64 us (5%)
  between operations  2.33 us (5%)
    pallas_call x1, Pallas kernels, local(): pl.pallas_call(kernel, name='chebyshev', out_shape=(pltpu.VMEM(shape, F32...  45.5 us
    unnamed x2, local copies, waits for them, and re-layouts  2.64 us

profile of v5, /device:TPU:1, one launch (start us, length us, event | category | flops | bytes accessed | tf_op | source)
XLA Modules:
  0.0 50.5 jit_solution(10423196421172897693)
XLA Ops:
  0.6 45.5 %chebyshev.1 = (f32[16,64,512]{2,1,0:T(8,128)S(1)}, f32[16,64,512]{2,1,0:T(8,128)S(1)}, f32[1,1]{1,0:T(1,128)}) custom-call(f32[16,64,512]{2,1,0:T(8,128)} %rhs.1, f32[16,64,512]{2,1,0:T(8,128)} %rea.1, f32[3,16,64,512]{3,2,1,0:T(8,128)} %vel.1), custom_call_target="tpu_custom_call" | custom-call | tf_op jit(solution)/shard_map/chebyshev/pallas_call | solution.py:417
  46.1 1.3 %copy.9 = f32[16,64,512]{2,1,0:T(8,128)} copy(f32[16,64,512]{2,1,0:T(8,128)S(1)} %get-tuple-element.9) | data formatting | bytes 4194304
  47.4 1.3 %copy.10 = f32[16,64,512]{2,1,0:T(8,128)} copy(f32[16,64,512]{2,1,0:T(8,128)S(1)} %get-tuple-element.10) | data formatting | bytes 4194304

commit v6 on v5

--- a/solution.py
+++ b/solution.py
@@ -25,7 +25,7 @@
 NXL, NYL, NT = 16, 64, 4
 NJ = NYL // 8
 TOP = 8
-NH = 2
+NH = 4
 CELLS = 256 * 256 * 1024
 SLABS = ((0, 1), (15, 1), (1, 4), (5, 4), (9, 6))
 
@@ -133,7 +133,7 @@
 
     def y_copies(buf, side, chunk):
         src, dst, to, _, _ = y_side[side]
-        if chunk == 0:
+        if isinstance(chunk, int) and chunk == 0:
             parts = [(pl.ds(2, NXL - 2), slice(None), 0)]
         else:
             parts = [(pl.ds(x, 1), pl.ds(tile(chunk - 1), 1), i) for i, x in enumerate((1, NXL))]
@@ -238,16 +238,17 @@
         down, up = pltpu.roll(m, 1, 1), pltpu.roll(m, 127, 1)
         before = pltpu.roll(now[x, jnp.maximum(at_t - 1, 0), rows, :], 1, 1)
         after = pltpu.roll(now[x, jnp.minimum(at_t + 1, NT - 1), rows, :], 127, 1)
-        if t == 0:
-            before, after = before * low, after * high
-        if t == NT - 1:
+        if isinstance(t, int):
             v = (x - 1) * NJ + j
             beyond = pltpu.roll(halo, (127 * (1 - gz) - v) & 127, 1)
             before = before * high + beyond * low
             after = after * low + beyond * high
+        else:
+            outer = jnp.where(t == 0, 1.0, 0.0)
+            before, after = before * (1.0 - outer * high), after * (1.0 - outer * low)
         zm = jnp.where(first_lane, before, down)
         zp = jnp.where(last_lane, after, up)
-        return cell_step(step, x, at_t, row, lines, m, zm, zp, sums, t)
+        return cell_step(step, x, at_t, row, lines, m, zm, zp, sums, j % NT)
 
     def cell_step(step, x, t, row, lines, m, zm, zp, sums, slot):
         now, new = D[step % 2], D[(step + 1) % 2]
@@ -300,10 +301,23 @@
 
         sums[:] = lax.fori_loop(0, count // many, body, tuple(sums))
 
-    def faces(step, t, h, sums=None):
-        js = range(h * (NJ // NH), (h + 1) * (NJ // NH))
-        halo = ZH[step % 2, 1]
-        late([functools.partial(face_group, step, x, j, t, halo, sums) for j in js for x in (1, NXL)])
+    def faces(step, t, sums):
+        cur, new, more = step % 2, (step + 1) % 2, step + 1 < ITERS
+        for h in range(NH):
+            x_each(cur, t, h, "wait_recv")
+            if h == 0:
+                y_each(cur, t + 1, "wait_recv", (1,))
+            if h == NH - 1:
+                y_each(cur, t + 1, "wait_recv", (0,))
+            js = range(h * (NJ // NH), (h + 1) * (NJ // NH))
+            halo = ZH[cur, 1] if isinstance(t, int) else None
+            late([functools.partial(face_group, step, x, j, t, halo, sums) for j in js for x in (1, NXL)])
+            if more:
+                x_each(new, t, h, "start")
+                if h == 0:
+                    y_each(new, t + 1, "start", (0,))
+                if h == NH - 1:
+                    y_each(new, t + 1, "start", (1,))
 
     for t, h in chunks:
         x_each(0, t, h, "start")
@@ -340,29 +354,19 @@
         if more:
             z_pack(new, 0)
             z_copy(new, 0).start()
-        for t, h in chunks:
-            x_each(cur, t, h, "wait_recv")
-            if h == 0:
-                y_each(cur, t + 1, "wait_recv", (1,))
-            if h == NH - 1:
-                y_each(cur, t + 1, "wait_recv", (0,))
-            if (t, h) == (NT - 1, 0):
-                z_copy(cur, 1).wait_recv()
-            faces(step, t, h, sums)
-            if more:
-                x_each(new, t, h, "start")
-                if h == 0:
-                    y_each(new, t + 1, "start", (0,))
-                if h == NH - 1:
-                    y_each(new, t + 1, "start", (1,))
-            place = t * NH + h
-            if place == 0:
-                z_copy(cur, 2).wait_recv()
-            if place < 3:
-                groups(step, [(10 + 2 * place + k, j) for k in range(2) for j in middle], ZH[cur, 2], sums)
-            if place == 3 and more:
-                z_pack(new, 2)
-                z_copy(new, 2).start()
+        def face_tile(t, carry):
+            part = list(carry)
+            faces(step, t, part)
+            pl.when(t == 0)(lambda: z_copy(cur, 2).wait_recv())
+            groups(step, [(10 + 2 * t + k, j) for k in range(2) for j in middle], ZH[cur, 2], part)
+            return tuple(part)
+
+        sums = list(lax.fori_loop(0, NT - 1, face_tile, tuple(sums)))
+        if more:
+            z_pack(new, 2)
+            z_copy(new, 2).start()
+        z_copy(cur, 1).wait_recv()
+        faces(step, NT - 1, sums)
         if more:
             z_pack(new, 1)
             z_copy(new, 1).start()
@@ -374,7 +378,7 @@
                 z_copy(cur, part).wait_send()
     total = jnp.sum((sums[0] + sums[1]) + (sums[2] + sums[3]), axis=0, keepdims=True)
 
-    def stage(total, G, send, recv, own, count, place):
+    def stage(total, G, send, recv, own, count, place, order, meanwhile):
         G[own, pl.ds(0, 1), :] = total
         copies = [
             pltpu.make_async_remote_copy(
@@ -385,10 +389,11 @@
                 device_id=place((own + o) % count),
                 device_id_type=MESH,
             )
-            for o in range(1, count)
+            for o in order
         ]
         for copy in copies:
             copy.start()
+        meanwhile()
         for copy in copies:
             copy.wait_recv()
         parts = [G[i, pl.ds(0, 1), :] for i in range(count)]
@@ -396,17 +401,20 @@
             parts = [a + b for a, b in zip(parts[::2], parts[1::2])]
         return parts[0], copies
 
-    total, c1 = stage(total, G1, g1s, g1r, gx, 16, lambda p: (p, gy, gz))
-    total, c2 = stage(total, G2, g2s, g2r, yz, 8, lambda p: (gx, p // 2, p % 2))
+    def last_sends():
+        cur = (ITERS - 1) % 2
+        for t, h in chunks:
+            x_each(cur, t, h, "wait_send")
+        for chunk in range(NT + 1):
+            y_each(cur, chunk, "wait_send")
+        for part in range(3):
+            z_copy(cur, part).wait_send()
+
+    far_first = (10, 6, 9, 11, 7, 5, 2, 14, 8, 3, 13, 1, 15, 4, 12)
+    total, c1 = stage(total, G1, g1s, g1r, gx, 16, lambda p: (p, gy, gz), far_first, last_sends)
+    total, c2 = stage(total, G2, g2s, g2r, yz, 8, lambda p: (gx, p // 2, p % 2), range(1, 8), lambda: None)
     whole = jnp.sum(total, axis=1, keepdims=True)
     norm[...] = jnp.sqrt(whole * (1.0 / CELLS) + 1e-06)
-    cur = (ITERS - 1) % 2
-    for t, h in chunks:
-        x_each(cur, t, h, "wait_send")
-    for chunk in range(NT + 1):
-        y_each(cur, chunk, "wait_send")
-    for part in range(3):
-        z_copy(cur, part).wait_send()
     for copy in c1 + c2:
         copy.wait_send()
 

time: 50.6 us -> 50.9 us (level)
  no operation moved by 1% of the time
where the time goes in v6:
time: 50.9 us; the launch traced here: 50.8 us
  Pallas kernels  45.8 us (90%)
  local copies, waits for them, and re-layouts  2.64 us (5%)
  between operations  2.33 us (5%)
    pallas_call x1, Pallas kernels, local(): pl.pallas_call(kernel, name='chebyshev', out_shape=(pltpu.VMEM(shape, F32...  45.8 us
    unnamed x2, local copies, waits for them, and re-layouts  2.64 us

profile of v6, /device:TPU:1, one launch (start us, length us, event | category | flops | bytes accessed | tf_op | source)
XLA Modules:
  0.0 50.8 jit_solution(3545666271311297070)
XLA Ops:
  0.6 45.8 %chebyshev.1 = (f32[16,64,512]{2,1,0:T(8,128)S(1)}, f32[16,64,512]{2,1,0:T(8,128)S(1)}, f32[1,1]{1,0:T(1,128)}) custom-call(f32[16,64,512]{2,1,0:T(8,128)} %rhs.1, f32[16,64,512]{2,1,0:T(8,128)} %rea.1, f32[3,16,64,512]{3,2,1,0:T(8,128)} %vel.1), custom_call_target="tpu_custom_call" | custom-call | tf_op jit(solution)/shard_map/chebyshev/pallas_call | solution.py:425
  46.5 1.3 %copy.9 = f32[16,64,512]{2,1,0:T(8,128)} copy(f32[16,64,512]{2,1,0:T(8,128)S(1)} %get-tuple-element.9) | data formatting | bytes 4194304
  47.8 1.3 %copy.10 = f32[16,64,512]{2,1,0:T(8,128)} copy(f32[16,64,512]{2,1,0:T(8,128)S(1)} %get-tuple-element.10) | data formatting | bytes 4194304

commit v7 on v6

--- a/solution.py
+++ b/solution.py
@@ -25,7 +25,7 @@
 NXL, NYL, NT = 16, 64, 4
 NJ = NYL // 8
 TOP = 8
-NH = 4
+NH = 2
 CELLS = 256 * 256 * 1024
 SLABS = ((0, 1), (15, 1), (1, 4), (5, 4), (9, 6))
 

time: 50.9 us -> 50.3 us (0.988)
  Pallas kernels: 45.8 us -> 45.2 us
    pallas_call x1, Pallas kernels: 45.8 us -> 45.2 us  [local(): pl.pallas_call(kernel, name='chebyshev', out_shape=(pltpu.VMEM(shape, F32...]
where the time goes in v7:
time: 50.3 us; the launch traced here: 50.1 us
  Pallas kernels  45.2 us (90%)
  local copies, waits for them, and re-layouts  2.64 us (5%)
  between operations  2.33 us (5%)
    pallas_call x1, Pallas kernels, local(): pl.pallas_call(kernel, name='chebyshev', out_shape=(pltpu.VMEM(shape, F32...  45.2 us
    unnamed x2, local copies, waits for them, and re-layouts  2.64 us

profile of v7, /device:TPU:1, one launch (start us, length us, event | category | flops | bytes accessed | tf_op | source)
XLA Modules:
  0.0 50.1 jit_solution(14396612258255256685)
XLA Ops:
  0.6 45.2 %chebyshev.1 = (f32[16,64,512]{2,1,0:T(8,128)S(1)}, f32[16,64,512]{2,1,0:T(8,128)S(1)}, f32[1,1]{1,0:T(1,128)}) custom-call(f32[16,64,512]{2,1,0:T(8,128)} %rhs.1, f32[16,64,512]{2,1,0:T(8,128)} %rea.1, f32[3,16,64,512]{3,2,1,0:T(8,128)} %vel.1), custom_call_target="tpu_custom_call" | custom-call | tf_op jit(solution)/shard_map/chebyshev/pallas_call | solution.py:425
  45.8 1.3 %copy.9 = f32[16,64,512]{2,1,0:T(8,128)} copy(f32[16,64,512]{2,1,0:T(8,128)S(1)} %get-tuple-element.9) | data formatting | bytes 4194304
  47.1 1.3 %copy.10 = f32[16,64,512]{2,1,0:T(8,128)} copy(f32[16,64,512]{2,1,0:T(8,128)S(1)} %get-tuple-element.10) | data formatting | bytes 4194304
